TPU v7x, 128 devices: a whole 4x4x4 slice. The times are simulated.
128 devices in a mesh: rep: 2 (over core), dp: 64 (over x, y, z).
Axes of the slice: x: 4, y: 4, z: 4, core: 2. Of those that a mesh axis runs over, the one named last changes fastest.
Arguments:
- x: bfloat16 [128, 2048, 768], P(('rep', 'dp')), parts along dimension 0
- dy: bfloat16 [128, 2048, 768], P(('rep', 'dp')), parts along dimension 0
- w_gate: bfloat16 [2, 768, 3072], replicated
- w_up: bfloat16 [2, 768, 3072], replicated
- w_down: bfloat16 [2, 3072, 768], replicated
- m_w_gate: float32 [2, 768, 3072], P(None, 'dp')
- m_w_up: float32 [2, 768, 3072], P(None, 'dp')
- m_w_down: float32 [2, 3072, 768], P(None, 'dp')
- v_w_gate: float32 [2, 768, 3072], P(None, 'dp')
- v_w_up: float32 [2, 768, 3072], P(None, 'dp')
- v_w_down: float32 [2, 3072, 768], P(None, 'dp')
Outputs:
- output 1: bfloat16 [4, 768, 3072], P('rep'), parts along dimension 0
- output 2: bfloat16 [4, 768, 3072], P('rep'), parts along dimension 0
- output 3: bfloat16 [4, 3072, 768], P('rep'), parts along dimension 0
- output 4: float32 [4, 768, 3072], P('rep', 'dp'), parts along dimension 0
- output 5: float32 [4, 768, 3072], P('rep', 'dp'), parts along dimension 0
- output 6: float32 [4, 3072, 768], P('rep', 'dp'), parts along dimension 0
- output 7: float32 [4, 768, 3072], P('rep', 'dp'), parts along dimension 0
- output 8: float32 [4, 768, 3072], P('rep', 'dp'), parts along dimension 0
- output 9: float32 [4, 3072, 768], P('rep', 'dp'), parts along dimension 0
There are 2 independent parts. A program takes and returns all parts, laid end to end along the dimension named above; an argument that names none is the same for every part.
All inputs are finite; a program needn't handle non-finite values.
Results may differ from a plain program's by a relative error of at most 0.022.
Values are sent between devices in bfloat16 or wider.
A program may use at most 1.5 GiB of HBM per device.

v0:
```python
import jax
import jax.numpy as jnp
from jax import lax

NAMES = ("w_gate", "w_up", "w_down")


def matmul(a, w):
    return jnp.dot(a, w, preferred_element_type=jnp.float32).astype(jnp.bfloat16)


def normed(h):
    wide = h.astype(jnp.float32)
    scale = lax.rsqrt(jnp.mean(wide**2, -1, keepdims=True) + 1e-6)
    return (wide * scale).astype(jnp.bfloat16)


def layer(h, w):
    a = normed(h)
    gate = jnp.dot(a, w["w_gate"], preferred_element_type=jnp.float32)
    up = jnp.dot(a, w["w_up"], preferred_element_type=jnp.float32)
    return h + matmul((jax.nn.silu(gate) * up).astype(jnp.bfloat16), w["w_down"])


def adamw(w, m, v, g):
    m = 0.9 * m + 0.1 * g
    v = 0.95 * v + 0.05 * g * g
    step = m * lax.rsqrt(v + 1e-8) + 0.1 * w
    return (w - 0.02 * step).astype(jnp.bfloat16), m, v


def stack(weights, h):
    for number in range(weights["w_gate"].shape[0]):
        h = layer(h, {name: w[number] for name, w in weights.items()})
    return h


def solution(mesh):
    groups = mesh.shape["rep"]

    def step(x, dy, *arrays):
        weights, m, v = (arrays[i : i + 3] for i in (0, 3, 6))
        x, dy = (t.reshape(groups, -1, *t.shape[1:]) for t in (x, dy))

        def of_a_group(x, dy):
            _, back = jax.vjp(lambda w: stack(w, x), dict(zip(NAMES, weights, strict=True)))
            by_weights = back(dy)[0]
            gradients = [by_weights[name].astype(jnp.float32) for name in NAMES]
            new = [adamw(w.astype(jnp.float32), m, v, g) for w, m, v, g in zip(weights, m, v, gradients, strict=True)]
            return tuple(one[which] for which in range(3) for one in new)

        return tuple(t.reshape(-1, *t.shape[2:]) for t in jax.vmap(of_a_group)(x, dy))

    return step
```

profile of v0, /device:TPU:0, one launch (start us, length us, event | category | flops | bytes accessed | tf_op | source)
XLA Modules:
  0.0 1486.2 jit_solution(6251239652480084547)
XLA Ops:
  7.2 2.7 fusion.39
  10.0 4.6 copy.11
  14.6 15.9 %fusion.71 = f32[2048,3072]{1,0:T(8,128)} fusion(bf16[2,768,3072]{2,1,0:T(8,128)(2,1)} %param, bf16[1,2048,768]{2,1,0:T(8,128)(2,1)S(1)} %copy-done.1, f32[2048]{0:T(1024)S(1)} %add_rsqrt_fusion), kind=kOutput, calls=%fused_computation.79 | convolution fusion | flops 9668395008 | bytes 33038336 | tf_op jit(solution)/vmap(jvp())/dot_general | solution.py:20
  30.5 15.9 %fusion.69 = f32[2048,3072]{1,0:T(8,128)} fusion(bf16[2,768,3072]{2,1,0:T(8,128)(2,1)} %param.3, bf16[1,2048,768]{2,1,0:T(8,128)(2,1)S(1)} %copy-done.1, f32[2048]{0:T(1024)S(1)} %add_rsqrt_fusion), kind=kOutput, calls=%fused_computation.77 | convolution fusion | flops 9668395008 | bytes 33038336 | tf_op jit(solution)/vmap(jvp())/dot_general | solution.py:21
  46.5 21.8 %fusion.30 = bf16[2048,3072]{1,0:T(8,128)(2,1)} fusion(f32[2048,3072]{1,0:T(8,128)} %fusion.69, f32[2048,3072]{1,0:T(8,128)} %fusion.71), kind=kLoop, calls=%fused_computation.35 | loop fusion | flops 37748736 | bytes 62914560
  68.3 15.1 %fusion.43 = (f32[2048]{0:T(1024)S(1)}, bf16[1,1,2048,768]{2,3,1,0:T(8,128)(2,1)S(1)}) fusion(bf16[2048,3072]{1,0:T(8,128)(2,1)} %fusion.30, bf16[2,3072,768]{2,1,0:T(8,128)(2,1)} %param.4, bf16[1,2048,768]{1,2,0:T(8,128)(2,1)S(1)} %copy-done.4), kind=kOutput, calls=%fused_computation.56 | convolution fusion | flops 9671538688 | bytes 23601152 | tf_op jit(solution)/vmap(jvp())/dot_general | solution.py:9
  84.1 16.2 %fusion.60 = f32[2048,3072]{1,0:T(8,128)} fusion(bf16[2,768,3072]{2,1,0:T(8,128)(2,1)} %param, bf16[1,1,2048,768]{2,3,1,0:T(8,128)(2,1)S(1)} %get-tuple-element.98, f32[2048]{0:T(1024)S(1)} %bitcast.401), kind=kOutput, calls=%fused_computation.68 | convolution fusion | flops 9668395008 | bytes 33038336 | tf_op jit(solution)/vmap(jvp())/dot_general | solution.py:20
  100.4 15.9 %fusion.63 = f32[2048,3072]{1,0:T(8,128)} fusion(bf16[2,768,3072]{2,1,0:T(8,128)(2,1)} %param.3, bf16[1,1,2048,768]{2,3,1,0:T(8,128)(2,1)S(1)} %get-tuple-element.98, f32[2048]{0:T(1024)S(1)} %bitcast.402), kind=kOutput, calls=%fused_computation.71 | convolution fusion | flops 9668395008 | bytes 33038336 | tf_op jit(solution)/vmap(jvp())/dot_general | solution.py:21
  116.2 14.9 convolution_convert_fusion.1
  131.1 3.2 copy.12
  134.3 21.1 %fusion.10 = bf16[2048,3072]{1,0:T(8,128)(2,1)S(1)} fusion(f32[2048,3072]{1,0:T(8,128)} %fusion.60, f32[2048,3072]{1,0:T(8,128)} %fusion.63, bf16[2048,3072]{1,0:T(8,128)(2,1)} %convolution_convert_fusion.1), kind=kLoop, calls=%fused_computation.11 | loop fusion | flops 75497472 | bytes 75497472
  155.4 4.6 copy-done
  160.0 12.5 fusion.85
  172.5 17.5 %fusion.45 = (f32[2048]{0:T(1024)S(1)}, bf16[2048,768]{0,1:T(8,128)(2,1)S(1)}) fusion(bf16[1,1,2048,768]{2,3,1,0:T(8,128)(2,1)S(1)} %copy-done.7, bf16[2048,768]{0,1:T(8,128)(2,1)S(1)} %fusion.85, bf16[2,768,3072]{2,1,0:T(8,128)(2,1)} %param.3, bf16[2048,3072]{1,0:T(8,128)(2,1)} %convolution_convert_fusion.1, f32[2048,3072]{1,0:T(8,128)} %fusion.60), kind=kOutput, calls=%fused_computation.58 | convolution fusion | flops 9710860288 | bytes 51912704 | tf_op jit(solution)/vmap(transpose(jvp()))/dot_general | solution.py:21
  194.0 15.6 %convolution_bitcast_fusion = f32[1,3072,768]{2,1,0:T(8,128)} fusion(bf16[2048,3072]{1,0:T(8,128)(2,1)} %fusion.30, bf16[2048,768]{0,1:T(8,128)(2,1)S(1)} %fusion.96), kind=kOutput, calls=%fused_computation.60 | convolution fusion | flops 9663676416 | bytes 25165824 | tf_op jit(solution)/vmap(transpose(jvp()))/dot_general | solution.py:9
  211.5 23.9 %fusion.46 = f32[1,3072,768]{2,1,0:T(8,128)} fusion(f32[2048,3072]{1,0:T(8,128)} %fusion.63, f32[2048,3072]{1,0:T(8,128)} %fusion.60, bf16[1,2048,768]{2,1,0:T(8,128)(2,1)S(1)} %copy-done.3), kind=kOutput, calls=%fused_computation.62 | convolution fusion | flops 9701425152 | bytes 62914560 | tf_op jit(solution)/vmap(transpose(jvp()))/dot_general | solution.py:9
  235.5 16.4 %convolution_convert_fusion = bf16[2048,3072]{1,0:T(8,128)(2,1)} fusion(bf16[2048,768]{0,1:T(8,128)(2,1)} %copy-done.9, bf16[2,3072,768]{2,1,0:T(8,128)(2,1)} %param.4), kind=kOutput, calls=%fused_computation.43 | convolution fusion | flops 9669967872 | bytes 20447232 | tf_op jit(solution)/vmap(transpose(jvp()))/dot_general | solution.py:9
  251.9 19.1 %fusion.55 = f32[1,768,3072]{2,1,0:T(8,128)} fusion(bf16[2048,3072]{1,0:T(8,128)(2,1)} %convolution_convert_fusion, f32[2048,3072]{1,0:T(8,128)} %fusion.71, bf16[1,2048,768]{1,2,0:T(8,128)(2,1)S(1)} %copy-done.5, f32[2048]{0:T(1024)S(1)} %copy-done.76), kind=kOutput, calls=%fused_computation.65 | convolution fusion | flops 9706143744 | bytes 50339840 | tf_op jit(solution)/vmap(transpose(jvp()))/dot_general | solution.py:21
  271.0 27.6 %fusion.52 = f32[1,768,3072]{2,1,0:T(8,128)} fusion(f32[2048,3072]{1,0:T(8,128)} %fusion.71, f32[2048,3072]{1,0:T(8,128)} %fusion.69, bf16[2048,3072]{1,0:T(8,128)(2,1)} %convolution_convert_fusion, bf16[1,2048,768]{1,2,0:T(8,128)(2,1)S(1)} %copy-done.5, f32[2048]{0:T(1024)S(1)} %copy-done.76), kind=kOutput, calls=%fused_computation.64 | convolution fusion | flops 9737601024 | bytes 75505664 | tf_op jit(solution)/vmap(transpose(jvp()))/dot_general | solution.py:20
  298.7 20.1 %fusion.49 = f32[1,768,3072]{2,1,0:T(8,128)} fusion(bf16[2048,3072]{1,0:T(8,128)(2,1)} %convolution_convert_fusion.1, f32[2048,3072]{1,0:T(8,128)} %fusion.60, bf16[1,1,2048,768]{2,3,1,0:T(8,128)(2,1)} %copy-done.6, f32[2048]{0:T(1024)S(1)} %bitcast.404), kind=kOutput, calls=%fused_computation.63 | convolution fusion | flops 9706143744 | bytes 50339840 | tf_op jit(solution)/vmap(transpose(jvp()))/dot_general | solution.py:21
  318.8 15.3 %convolution_bitcast_fusion.1 = f32[1,768,3072]{2,1,0:T(8,128)} fusion(bf16[2048,3072]{1,0:T(8,128)(2,1)} %copy-done, bf16[1,1,2048,768]{2,3,1,0:T(8,128)(2,1)S(1)} %copy-done.8, f32[2048]{0:T(1024)S(1)} %bitcast.405), kind=kOutput, calls=%fused_computation.61 | convolution fusion | flops 9668395008 | bytes 25174016 | tf_op jit(solution)/vmap(transpose(jvp()))/dot_general | solution.py:20
  334.0 565.1 %fusion.151 = (f32[16,3072]{1,0:T(8,128)S(1)}, f32[16,3072]{1,0:T(8,128)S(1)}, f32[16,3072]{1,0:T(8,128)S(1)}, f32[16,3072]{1,0:T(8,128)S(1)}) fusion(f32[1,768,3072]{2,1,0:T(8,128)} %fusion.52, f32[1,768,3072]{2,1,0:T(8,128)} %convolution_bitcast_fusion.1, f32[1,768,3072]{2,1,0:T(8,128)} %fusion.55, f32[1,768,3072]{2,1,0:T(8,128)} %fusion.49), kind=kCustom, calls=%all-reduce-scatter.4 | all-reduce-scatter fusion | flops 12582913 | bytes 38535680
  900.8 3.5 collective-permute-start.31
  904.3 3.7 collective-permute-start.47
  912.9 7.0 collective-permute-start.10
  922.0 3.2 collective-permute-start.12
  925.3 2.7 collective-permute-start.13
  928.1 3.2 collective-permute-start.14
  935.4 3.3 collective-permute-start.4
  938.8 4.7 collective-permute-start.5
  943.5 2.8 collective-permute-start.6
  946.3 3.4 collective-permute-start.7
  951.9 3.8 collective-permute-start.9
  957.8 3.5 collective-permute-start.17
  961.4 2.5 collective-permute-start.18
  963.8 2.4 collective-permute-start.19
  968.4 4.3 collective-permute-start.21
  972.7 3.1 collective-permute-start.22
  975.8 2.6 collective-permute-start.23
  979.7 3.0 collective-permute-start.25
  987.4 2.4 collective-permute-start.29
  994.2 6.0 collective-permute-start.33
  1000.3 4.5 collective-permute-start.34
  1008.0 5.0 collective-permute-start.37
  1013.1 3.9 collective-permute-start.38
  1020.4 3.4 collective-permute-start.41
  1031.0 2.5 collective-permute-start.46
  1033.5 2.8 collective-permute-start.48
  1036.3 2.8 collective-permute-start.49
  1039.1 4.3 collective-permute-start.50
  1043.5 3.4 collective-permute-start.51
  1049.1 3.9 collective-permute-start.53
  1053.1 4.0 collective-permute-start.54
  1060.6 3.4 collective-permute-start.57
  1076.1 27.5 %concatenate = bf16[268,3072]{1,0:T(8,128)(2,1)S(1)} concatenate(bf16[12,3072]{1,0:T(8,128)(2,1)} %copy-done.15, bf16[16,3072]{1,0:T(8,128)(2,1)} %copy-done.22, bf16[16,3072]{1,0:T(8,128)(2,1)} %copy-done.21, bf16[16,3072]{1,0:T(8,128)(2,1)} %copy-done.20, bf16[16,3072]{1,0:T(8,128)(2,1)} %copy-done.19, bf16[16,3072]{1,0:T(8,128)(2,1)} %copy-done.18, ...), dimensions={0} | concatenate | bytes 3391488
  1103.6 39.9 %concatenate.1 = bf16[268,3072]{1,0:T(8,128)(2,1)} concatenate(bf16[12,3072]{1,0:T(8,128)(2,1)} %copy-done.14, bf16[16,3072]{1,0:T(8,128)(2,1)} %copy-done.45, bf16[16,3072]{1,0:T(8,128)(2,1)} %copy-done.44, bf16[16,3072]{1,0:T(8,128)(2,1)} %copy-done.43, bf16[16,3072]{1,0:T(8,128)(2,1)} %copy-done.42, bf16[16,3072]{1,0:T(8,128)(2,1)} %copy-done.41, bf16[16,3072]{1,0:T(8,128)(2,1)} %copy-done.40, ...), dimensions={0} | concatenate | bytes 3391488
  1143.5 39.9 %concatenate.2 = bf16[268,3072]{1,0:T(8,128)(2,1)} concatenate(bf16[12,3072]{1,0:T(8,128)(2,1)} %copy-done.13, bf16[16,3072]{1,0:T(8,128)(2,1)} %copy-done.62, bf16[16,3072]{1,0:T(8,128)(2,1)} %copy-done.60, bf16[16,3072]{1,0:T(8,128)(2,1)} %copy-done.58, bf16[16,3072]{1,0:T(8,128)(2,1)} %copy-done.57, bf16[16,3072]{1,0:T(8,128)(2,1)} %copy-done.56, bf16[16,3072]{1,0:T(8,128)(2,1)} %copy-done.55, ...), dimensions={0} | concatenate | bytes 3391488
  1183.4 39.0 %concatenate.3 = bf16[268,3072]{1,0:T(8,128)(2,1)} concatenate(bf16[12,3072]{1,0:T(8,128)(2,1)S(1)} %collective-permute-done.63, bf16[16,3072]{1,0:T(8,128)(2,1)} %collective-permute-done.62, bf16[16,3072]{1,0:T(8,128)(2,1)} %collective-permute-done.61, bf16[16,3072]{1,0:T(8,128)(2,1)} %collective-permute-done.60, bf16[16,3072]{1,0:T(8,128)(2,1)} %collective-permute-done.59, ...), dimensions={0} | concatenate | bytes 3391488
  1237.1 66.6 %all-gather.10.cloned.1.call-done = bf16[1,2,768,3072]{3,1,0,2:T(2,128)(2,1)} async-done(((bf16[1,2,12,3072]{3,1,0,2:T(2,128)(2,1)}), bf16[1,2,768,3072]{3,1,0,2:T(2,128)(2,1)}) %all-gather.10.cloned.1.call-update) | async-done | bytes 9437200 | tf_op jit(solution)/reshape | solution.py:52
  1303.6 10.4 copy.18
  1314.0 73.7 %all-gather.12.cloned.1.call-done = bf16[1,2,768,3072]{3,1,0,2:T(2,128)(2,1)} async-done(((bf16[1,2,12,3072]{3,1,0,2:T(2,128)(2,1)}), bf16[1,2,768,3072]{3,1,0,2:T(2,128)(2,1)}) %all-gather.12.cloned.1.call-update) | async-done | bytes 9437200 | tf_op jit(solution)/reshape | solution.py:52
  1387.7 10.3 copy.19
  1398.0 73.1 %all-gather.14.cloned.1.call-done = bf16[1,2,3072,768]{3,2,1,0:T(8,128)(2,1)} async-done(((bf16[1,2,48,768]{3,2,1,0:T(8,128)(2,1)}), bf16[1,2,3072,768]{3,2,1,0:T(8,128)(2,1)}) %all-gather.14.cloned.1.call-update) | async-done | bytes 9437200 | tf_op jit(solution)/reshape | solution.py:52
  1471.2 8.0 copy.61
  (291 shorter events, 79.9 us)
Async XLA Ops:
  7.2 1222.1 %reduce-scatter.25.cloned.1.call-start = ((), (), s32[]{:S(2)}) async-start(), calls=%async_computation.6 | async-start | bytes 9584640
  209.6 1020.7 %reduce-scatter.23.cloned.1.call-start = ((), (), s32[]{:S(2)}) async-start(), calls=%async_computation.5 | async-start | bytes 9584640
  235.5 1068.2 %all-gather.10.cloned.1.call-start = ((), (), s32[]{:S(2)}) async-start(), calls=%async_computation.2 | async-start | bytes 9584640 | tf_op jit(solution)/reshape | solution.py:52
  899.2 12.3 collective-permute-start.15
  900.8 12.1 collective-permute-start.31
  904.3 15.6 %collective-permute-start.47 = (bf16[12,3072]{1,0:T(8,128)(2,1)S(1)}, bf16[12,3072]{1,0:T(8,128)(2,1)S(1)}, u32[]{:S(2)}, u32[]{:S(2)}) collective-permute-start(bf16[12,3072]{1,0:T(8,128)(2,1)S(1)} %slice.26), channel_id=1, source_target_pairs={{0,16},{1,17},{2,18},{3,19},{4,20},{5,21},{6,22},{7,23},{8,24},{9,... | collective-permute-start | bytes 221192
  908.0 14.0 collective-permute-start.63
  910.0 15.3 %collective-permute-start = (bf16[16,3072]{1,0:T(8,128)(2,1)S(1)}, bf16[16,3072]{1,0:T(8,128)(2,1)S(1)}, u32[]{:S(2)}, u32[]{:S(2)}) collective-permute-start(bf16[16,3072]{1,0:T(8,128)(2,1)S(1)} %convert.168), channel_id=1, source_target_pairs={{0,1},{1,2},{2,3},{3,4},{4,5},{5,6},{6,7},{7,8},{8,9},{9,10},{10,1... | collective-permute-start | bytes 294920
  911.6 16.5 %collective-permute-start.1 = (bf16[16,3072]{1,0:T(8,128)(2,1)S(1)}, bf16[16,3072]{1,0:T(8,128)(2,1)S(1)}, u32[]{:S(2)}, u32[]{:S(2)}) collective-permute-start(bf16[16,3072]{1,0:T(8,128)(2,1)S(1)} %convert.168), channel_id=1, source_target_pairs={{0,2},{1,3},{2,4},{3,5},{4,6},{5,7},{6,8},{7,9},{8,10},{9,11},{10,... | collective-permute-start | bytes 294920
  912.9 18.4 %collective-permute-start.10 = (bf16[16,3072]{1,0:T(8,128)(2,1)S(1)}, bf16[16,3072]{1,0:T(8,128)(2,1)S(1)}, u32[]{:S(2)}, u32[]{:S(2)}) collective-permute-start(bf16[16,3072]{1,0:T(8,128)(2,1)S(1)} %convert.168), channel_id=1, source_target_pairs={{0,11},{1,12},{2,13},{3,14},{4,15},{5,16},{6,17},{7,18},{8,19},{9,... | collective-permute-start | bytes 294920
  919.9 13.5 collective-permute-start.11
  922.0 13.4 collective-permute-start.12
  925.3 13.4 collective-permute-start.13
  928.1 15.4 %collective-permute-start.14 = (bf16[16,3072]{1,0:T(8,128)(2,1)S(1)}, bf16[16,3072]{1,0:T(8,128)(2,1)S(1)}, u32[]{:S(2)}, u32[]{:S(2)}) collective-permute-start(bf16[16,3072]{1,0:T(8,128)(2,1)S(1)} %convert.168), channel_id=1, source_target_pairs={{0,15},{1,16},{2,17},{3,18},{4,19},{5,20},{6,21},{7,22},{8,23},{9,... | collective-permute-start | bytes 294920
  931.3 14.9 %collective-permute-start.2 = (bf16[16,3072]{1,0:T(8,128)(2,1)S(1)}, bf16[16,3072]{1,0:T(8,128)(2,1)S(1)}, u32[]{:S(2)}, u32[]{:S(2)}) collective-permute-start(bf16[16,3072]{1,0:T(8,128)(2,1)S(1)} %convert.168), channel_id=1, source_target_pairs={{0,3},{1,4},{2,5},{3,6},{4,7},{5,8},{6,9},{7,10},{8,11},{9,12},{10... | collective-permute-start | bytes 294920
  933.4 16.3 %collective-permute-start.3 = (bf16[16,3072]{1,0:T(8,128)(2,1)S(1)}, bf16[16,3072]{1,0:T(8,128)(2,1)S(1)}, u32[]{:S(2)}, u32[]{:S(2)}) collective-permute-start(bf16[16,3072]{1,0:T(8,128)(2,1)S(1)} %convert.168), channel_id=1, source_target_pairs={{0,4},{1,5},{2,6},{3,7},{4,8},{5,9},{6,10},{7,11},{8,12},{9,13},{1... | collective-permute-start | bytes 294920
  935.4 16.5 %collective-permute-start.4 = (bf16[16,3072]{1,0:T(8,128)(2,1)S(1)}, bf16[16,3072]{1,0:T(8,128)(2,1)S(1)}, u32[]{:S(2)}, u32[]{:S(2)}) collective-permute-start(bf16[16,3072]{1,0:T(8,128)(2,1)S(1)} %convert.168), channel_id=1, source_target_pairs={{0,5},{1,6},{2,7},{3,8},{4,9},{5,10},{6,11},{7,12},{8,13},{9,14},{... | collective-permute-start | bytes 294920
  938.8 16.9 %collective-permute-start.5 = (bf16[16,3072]{1,0:T(8,128)(2,1)S(1)}, bf16[16,3072]{1,0:T(8,128)(2,1)S(1)}, u32[]{:S(2)}, u32[]{:S(2)}) collective-permute-start(bf16[16,3072]{1,0:T(8,128)(2,1)S(1)} %convert.168), channel_id=1, source_target_pairs={{0,6},{1,7},{2,8},{3,9},{4,10},{5,11},{6,12},{7,13},{8,14},{9,15},... | collective-permute-start | bytes 294920
  943.5 14.3 collective-permute-start.6
  946.3 15.1 %collective-permute-start.7 = (bf16[16,3072]{1,0:T(8,128)(2,1)S(1)}, bf16[16,3072]{1,0:T(8,128)(2,1)S(1)}, u32[]{:S(2)}, u32[]{:S(2)}) collective-permute-start(bf16[16,3072]{1,0:T(8,128)(2,1)S(1)} %convert.168), channel_id=1, source_target_pairs={{0,8},{1,9},{2,10},{3,11},{4,12},{5,13},{6,14},{7,15},{8,16},{9,17... | collective-permute-start | bytes 294920
  949.7 14.1 collective-permute-start.8
  951.9 14.4 collective-permute-start.9
  955.7 12.6 collective-permute-start.16
  957.8 14.9 %collective-permute-start.17 = (bf16[16,3072]{1,0:T(8,128)(2,1)S(1)}, bf16[16,3072]{1,0:T(8,128)(2,1)S(1)}, u32[]{:S(2)}, u32[]{:S(2)}) collective-permute-start(bf16[16,3072]{1,0:T(8,128)(2,1)S(1)} %convert.169), channel_id=1, source_target_pairs={{0,2},{1,3},{2,4},{3,5},{4,6},{5,7},{6,8},{7,9},{8,10},{9,11},{10,... | collective-permute-start | bytes 294920
  961.4 14.4 collective-permute-start.18
  963.8 14.6 collective-permute-start.19
  966.3 13.4 collective-permute-start.20
  968.4 14.4 collective-permute-start.21
  972.7 12.0 collective-permute-start.22
  975.8 10.2 collective-permute-start.23
  979.7 10.0 collective-permute-start.25
  986.0 14.2 collective-permute-start.28
  987.4 17.4 %collective-permute-start.29 = (bf16[16,3072]{1,0:T(8,128)(2,1)S(1)}, bf16[16,3072]{1,0:T(8,128)(2,1)S(1)}, u32[]{:S(2)}, u32[]{:S(2)}) collective-permute-start(bf16[16,3072]{1,0:T(8,128)(2,1)S(1)} %convert.169), channel_id=1, source_target_pairs={{0,14},{1,15},{2,16},{3,17},{4,18},{5,19},{6,20},{7,21},{8,22},{9,... | collective-permute-start | bytes 294920
  990.5 15.6 %collective-permute-start.30 = (bf16[16,3072]{1,0:T(8,128)(2,1)S(1)}, bf16[16,3072]{1,0:T(8,128)(2,1)S(1)}, u32[]{:S(2)}, u32[]{:S(2)}) collective-permute-start(bf16[16,3072]{1,0:T(8,128)(2,1)S(1)} %convert.169), channel_id=1, source_target_pairs={{0,15},{1,16},{2,17},{3,18},{4,19},{5,20},{6,21},{7,22},{8,23},{9,... | collective-permute-start | bytes 294920
  992.1 15.9 %collective-permute-start.32 = (bf16[16,3072]{1,0:T(8,128)(2,1)S(1)}, bf16[16,3072]{1,0:T(8,128)(2,1)S(1)}, u32[]{:S(2)}, u32[]{:S(2)}) collective-permute-start(bf16[16,3072]{1,0:T(8,128)(2,1)S(1)} %convert.166), channel_id=1, source_target_pairs={{0,1},{1,2},{2,3},{3,4},{4,5},{5,6},{6,7},{7,8},{8,9},{9,10},{10,1... | collective-permute-start | bytes 294920
  994.2 18.8 %collective-permute-start.33 = (bf16[16,3072]{1,0:T(8,128)(2,1)S(1)}, bf16[16,3072]{1,0:T(8,128)(2,1)S(1)}, u32[]{:S(2)}, u32[]{:S(2)}) collective-permute-start(bf16[16,3072]{1,0:T(8,128)(2,1)S(1)} %convert.166), channel_id=1, source_target_pairs={{0,2},{1,3},{2,4},{3,5},{4,6},{5,7},{6,8},{7,9},{8,10},{9,11},{10,... | collective-permute-start | bytes 294920
  1000.3 16.7 %collective-permute-start.34 = (bf16[16,3072]{1,0:T(8,128)(2,1)S(1)}, bf16[16,3072]{1,0:T(8,128)(2,1)S(1)}, u32[]{:S(2)}, u32[]{:S(2)}) collective-permute-start(bf16[16,3072]{1,0:T(8,128)(2,1)S(1)} %convert.166), channel_id=1, source_target_pairs={{0,3},{1,4},{2,5},{3,6},{4,7},{5,8},{6,9},{7,10},{8,11},{9,12},{10... | collective-permute-start | bytes 294920
  1004.8 13.6 collective-permute-start.35
  1006.1 14.3 collective-permute-start.36
  1008.0 15.8 %collective-permute-start.37 = (bf16[16,3072]{1,0:T(8,128)(2,1)S(1)}, bf16[16,3072]{1,0:T(8,128)(2,1)S(1)}, u32[]{:S(2)}, u32[]{:S(2)}) collective-permute-start(bf16[16,3072]{1,0:T(8,128)(2,1)S(1)} %convert.166), channel_id=1, source_target_pairs={{0,6},{1,7},{2,8},{3,9},{4,10},{5,11},{6,12},{7,13},{8,14},{9,15},... | collective-permute-start | bytes 294920
  1013.1 12.1 collective-permute-start.38
  1020.4 9.8 collective-permute-start.41
  1023.9 9.6 collective-permute-start.42
  1025.2 11.0 collective-permute-start.43
  1026.5 12.6 collective-permute-start.44
  1027.9 15.6 %collective-permute-start.45 = (bf16[16,3072]{1,0:T(8,128)(2,1)S(1)}, bf16[16,3072]{1,0:T(8,128)(2,1)S(1)}, u32[]{:S(2)}, u32[]{:S(2)}) collective-permute-start(bf16[16,3072]{1,0:T(8,128)(2,1)S(1)} %convert.166), channel_id=1, source_target_pairs={{0,14},{1,15},{2,16},{3,17},{4,18},{5,19},{6,20},{7,21},{8,22},{9,... | collective-permute-start | bytes 294920
  1031.0 15.9 %collective-permute-start.46 = (bf16[16,3072]{1,0:T(8,128)(2,1)S(1)}, bf16[16,3072]{1,0:T(8,128)(2,1)S(1)}, u32[]{:S(2)}, u32[]{:S(2)}) collective-permute-start(bf16[16,3072]{1,0:T(8,128)(2,1)S(1)} %convert.166), channel_id=1, source_target_pairs={{0,15},{1,16},{2,17},{3,18},{4,19},{5,20},{6,21},{7,22},{8,23},{9,... | collective-permute-start | bytes 294920
  1033.5 15.6 %collective-permute-start.48 = (bf16[16,3072]{1,0:T(8,128)(2,1)S(1)}, bf16[16,3072]{1,0:T(8,128)(2,1)S(1)}, u32[]{:S(2)}, u32[]{:S(2)}) collective-permute-start(bf16[16,3072]{1,0:T(8,128)(2,1)S(1)} %convert.167), channel_id=1, source_target_pairs={{0,1},{1,2},{2,3},{3,4},{4,5},{5,6},{6,7},{7,8},{8,9},{9,10},{10,1... | collective-permute-start | bytes 294920
  1036.3 16.8 %collective-permute-start.49 = (bf16[16,3072]{1,0:T(8,128)(2,1)S(1)}, bf16[16,3072]{1,0:T(8,128)(2,1)S(1)}, u32[]{:S(2)}, u32[]{:S(2)}) collective-permute-start(bf16[16,3072]{1,0:T(8,128)(2,1)S(1)} %convert.167), channel_id=1, source_target_pairs={{0,2},{1,3},{2,4},{3,5},{4,6},{5,7},{6,8},{7,9},{8,10},{9,11},{10,... | collective-permute-start | bytes 294920
  1039.1 18.0 %collective-permute-start.50 = (bf16[16,3072]{1,0:T(8,128)(2,1)S(1)}, bf16[16,3072]{1,0:T(8,128)(2,1)S(1)}, u32[]{:S(2)}, u32[]{:S(2)}) collective-permute-start(bf16[16,3072]{1,0:T(8,128)(2,1)S(1)} %convert.167), channel_id=1, source_target_pairs={{0,3},{1,4},{2,5},{3,6},{4,7},{5,8},{6,9},{7,10},{8,11},{9,12},{10... | collective-permute-start | bytes 294920
  1043.5 15.0 %collective-permute-start.51 = (bf16[16,3072]{1,0:T(8,128)(2,1)S(1)}, bf16[16,3072]{1,0:T(8,128)(2,1)S(1)}, u32[]{:S(2)}, u32[]{:S(2)}) collective-permute-start(bf16[16,3072]{1,0:T(8,128)(2,1)S(1)} %convert.167), channel_id=1, source_target_pairs={{0,4},{1,5},{2,6},{3,7},{4,8},{5,9},{6,10},{7,11},{8,12},{9,13},{1... | collective-permute-start | bytes 294920
  1046.9 13.7 collective-permute-start.52
  1049.1 14.9 %collective-permute-start.53 = (bf16[16,3072]{1,0:T(8,128)(2,1)S(1)}, bf16[16,3072]{1,0:T(8,128)(2,1)S(1)}, u32[]{:S(2)}, u32[]{:S(2)}) collective-permute-start(bf16[16,3072]{1,0:T(8,128)(2,1)S(1)} %convert.167), channel_id=1, source_target_pairs={{0,6},{1,7},{2,8},{3,9},{4,10},{5,11},{6,12},{7,13},{8,14},{9,15},... | collective-permute-start | bytes 294920
  1053.1 12.9 collective-permute-start.54
  1057.1 10.8 collective-permute-start.55
  1058.5 11.4 collective-permute-start.56
  1060.6 11.2 collective-permute-start.57
  1064.1 119.3 %collective-permute-start.58 = (bf16[16,3072]{1,0:T(8,128)(2,1)S(1)}, bf16[16,3072]{1,0:T(8,128)(2,1)}, u32[]{:S(2)}, u32[]{:S(2)}) collective-permute-start(bf16[16,3072]{1,0:T(8,128)(2,1)S(1)} %convert.167), channel_id=1, source_target_pairs={{0,11},{1,12},{2,13},{3,14},{4,15},{5,16},{6,17},{7,18},{8,19},{9,... | collective-permute-start | bytes 294920
  1066.0 117.4 %collective-permute-start.59 = (bf16[16,3072]{1,0:T(8,128)(2,1)S(1)}, bf16[16,3072]{1,0:T(8,128)(2,1)}, u32[]{:S(2)}, u32[]{:S(2)}) collective-permute-start(bf16[16,3072]{1,0:T(8,128)(2,1)S(1)} %convert.167), channel_id=1, source_target_pairs={{0,12},{1,13},{2,14},{3,15},{4,16},{5,17},{6,18},{7,19},{8,20},{9,... | collective-permute-start | bytes 294920
  1067.9 115.4 %collective-permute-start.60 = (bf16[16,3072]{1,0:T(8,128)(2,1)S(1)}, bf16[16,3072]{1,0:T(8,128)(2,1)}, u32[]{:S(2)}, u32[]{:S(2)}) collective-permute-start(bf16[16,3072]{1,0:T(8,128)(2,1)S(1)} %convert.167), channel_id=1, source_target_pairs={{0,13},{1,14},{2,15},{3,16},{4,17},{5,18},{6,19},{7,20},{8,21},{9,... | collective-permute-start | bytes 294920
  1069.8 113.5 %collective-permute-start.61 = (bf16[16,3072]{1,0:T(8,128)(2,1)S(1)}, bf16[16,3072]{1,0:T(8,128)(2,1)}, u32[]{:S(2)}, u32[]{:S(2)}) collective-permute-start(bf16[16,3072]{1,0:T(8,128)(2,1)S(1)} %convert.167), channel_id=1, source_target_pairs={{0,14},{1,15},{2,16},{3,17},{4,18},{5,19},{6,20},{7,21},{8,22},{9,... | collective-permute-start | bytes 294920
  1071.8 111.6 %collective-permute-start.62 = (bf16[16,3072]{1,0:T(8,128)(2,1)S(1)}, bf16[16,3072]{1,0:T(8,128)(2,1)}, u32[]{:S(2)}, u32[]{:S(2)}) collective-permute-start(bf16[16,3072]{1,0:T(8,128)(2,1)S(1)} %convert.167), channel_id=1, source_target_pairs={{0,15},{1,16},{2,17},{3,18},{4,19},{5,20},{6,21},{7,22},{8,23},{9,... | collective-permute-start | bytes 294920
  1228.0 159.7 %all-gather.12.cloned.1.call-start = ((), (), s32[]{:S(2)}) async-start(), calls=%async_computation.3 | async-start | bytes 9584640 | tf_op jit(solution)/reshape | solution.py:52
  1228.9 242.2 %all-gather.14.cloned.1.call-start = ((), (), s32[]{:S(2)}) async-start(), calls=%async_computation.4 | async-start | bytes 9584640 | tf_op jit(solution)/reshape | solution.py:52
  (83 other events, 5234.5 us)
Sparse Core Ops, SparseCore 0:
  209.7 709.6 reduce-scatter.24
  924.0 253.7 reduce-scatter.22
  1228.2 75.4 all-gather.9
  1306.9 80.7 all-gather.11
  1390.4 80.7 all-gather.13
where the time goes:
time: 1500 us; the launch traced here: 1490 us
  blocking collectives  565 us (38%)
  matrix products  262 us (17%)
  waiting for transfers between devices  214 us (14%)
  local copies, waits for them, and re-layouts  202 us (13%)
  starting transfers between devices  172 us (11%)
  other arithmetic  53.8 us (4%)
  between operations  17.8 us (1%)
    unnamed x1, blocking collectives  565 us
    reshape x3, waiting for transfers between devices, step(): t.reshape(-1, *t.shape[2:])  213 us
    unnamed x174, local copies, waits for them, and re-layouts  198 us
    unnamed x66, starting transfers between devices  171 us
    dot_general x5, matrix products, layer(): up = jnp.dot(a, w['w_up'], preferred_element_type=jnp.float32)  88.6 us
    dot_general x5, matrix products, layer(): gate = jnp.dot(a, w['w_gate'], preferred_element_type=jnp.float32)  87.5 us
    dot_general x5, matrix products, matmul(): jnp.dot(a, w, preferred_element_type=jnp.float32).astype(jnp.bfloat16)  85.8 us
    unnamed x7, other arithmetic  45.2 us
  transfers between devices with their start and end apart: 69, of which 3 were waited for; matrix products, arithmetic and copies ran while one was open for 59% of the time, Pallas kernels for 0%

commit v1 on v0

v1 whole, which is shorter than its diff:
```python
import functools

import jax
import jax.numpy as jnp
from jax import lax
from jax.experimental import pallas as pl
from jax.experimental.pallas import tpu as pltpu
from jax.sharding import PartitionSpec as P

F32 = jnp.float32
BF16 = jnp.bfloat16
MESH = pl.DeviceIdType.MESH
ANY = pl.BlockSpec(memory_space=pl.ANY)
VMEM = pl.BlockSpec(memory_space=pltpu.VMEM)
STRIDE = (16, 4, 1)
ORDER = ((0, 1, 2), (1, 2, 0), (2, 0, 1))
VMEM_LIMIT = 60 * 1024 * 1024


def matmul(a, w):
    return jnp.dot(a, w, preferred_element_type=F32).astype(BF16)


def over_tokens(a, b):
    return lax.dot_general(a, b, (((0,), (0,)), ((), ())), preferred_element_type=F32)


def wide_kernel(a_ref, d_ref, out_ref, s_ref):
    s_ref[...] = over_tokens(a_ref[...], d_ref[...])

    def two_devices(i, _):
        rows = s_ref[pl.ds(pl.multiple_of(24 * i, 8), 24), :]
        for k in range(2):
            block = [rows[12 * k : 12 * k + 12, 128 * q : 128 * q + 128] for q in range(4)]
            out_ref[0, 2 * i + k] = jnp.concatenate(block, axis=0).astype(BF16)
        return 0

    lax.fori_loop(0, 32, two_devices, 0)


def wide_gradient(a, d):
    tokens, rows = a.shape
    return pl.pallas_call(
        wide_kernel,
        grid=(6,),
        in_specs=[pl.BlockSpec((tokens, rows), lambda j: (0, 0)), pl.BlockSpec((tokens, 512), lambda j: (0, j))],
        out_specs=pl.BlockSpec((1, 64, 48, 128), lambda j: (j, 0, 0, 0)),
        out_shape=jax.ShapeDtypeStruct((6, 64, 48, 128), BF16),
        scratch_shapes=[pltpu.VMEM((rows, 512), F32)],
        compiler_params=pltpu.CompilerParams(vmem_limit_bytes=VMEM_LIMIT),
        cost_estimate=pl.CostEstimate(flops=2 * tokens * rows * 3072, bytes_accessed=20 << 20, transcendentals=0),
    )(a, d)


def down_kernel(act_ref, d_ref, out_ref):
    total = over_tokens(act_ref[...], d_ref[...])
    for j in range(6):
        out_ref[j] = total[:, 128 * j : 128 * j + 128].astype(BF16)


def down_gradient(act, d):
    tokens, columns = d.shape
    out = pl.pallas_call(
        down_kernel,
        grid=(6,),
        in_specs=[pl.BlockSpec((tokens, 512), lambda i: (0, i)), pl.BlockSpec((tokens, columns), lambda i: (0, 0))],
        out_specs=pl.BlockSpec((6, 512, 128), lambda i: (0, i, 0)),
        out_shape=jax.ShapeDtypeStruct((6, 3072, 128), BF16),
        compiler_params=pltpu.CompilerParams(vmem_limit_bytes=VMEM_LIMIT),
        cost_estimate=pl.CostEstimate(flops=2 * tokens * columns * 3072, bytes_accessed=20 << 20, transcendentals=0),
    )(act, d)
    return out.reshape(6, 64, 48, 128)


def adamw(w, m, v, g):
    m = 0.9 * m + 0.1 * g
    v = 0.95 * v + 0.05 * g * g
    step = m * lax.rsqrt(v + 1e-8) + 0.1 * w
    return w - 0.02 * step, m, v


class Exchange:
    def __init__(self, number, g_refs, w_refs, m_refs, v_refs, sum_ref, full_ref, out_ref, bufs, own, scratch, sems):
        self.number, self.g, self.w, self.m, self.v = number, g_refs, w_refs, m_refs, v_refs
        self.sum, self.full, self.out, self.bufs, self.own, self.scratch = sum_ref, full_ref, out_ref, bufs, own, scratch
        self.send_sem, self.recv_sem, self.own_sem, self.out_sem = sems
        me = lax.axis_index("dp")
        self.at = (me // 16, (me // 4) % 4, me % 4)
        self.right = tuple(me + STRIDE[a] * ((self.at[a] + 1) % 4 - self.at[a]) for a in range(3))
        self.left = tuple(me + STRIDE[a] * ((self.at[a] + 3) % 4 - self.at[a]) for a in range(3))

    def barrier(self):
        barrier = pltpu.get_barrier_semaphore()
        for axis in range(3):
            for to in (self.left[axis], self.right[axis]):
                pl.semaphore_signal(barrier, inc=1, device_id={"dp": to}, device_id_type=MESH)
        pl.semaphore_wait(barrier, 6)

    def copy(self, key, src, dst, to):
        m, c, phase, which = key
        n = 6 * phase + which
        return pltpu.make_async_remote_copy(
            src_ref=src,
            dst_ref=dst,
            send_sem=self.send_sem.at[3 * m + c, n],
            recv_sem=self.recv_sem.at[3 * m + c, n],
            device_id={"dp": to},
            device_id_type=MESH,
        )

    def block(self, m, c, phase, half, k):
        axis = ORDER[c][phase]
        place = sorted(ORDER[c][phase:]).index(axis)
        where = (slice(None),) * place + (k,)
        if phase == 0:
            return self.g[m].at[(2 * c + half, *where)]
        return self.bufs[phase - 1][1].at[(m, c, half, *where)]

    def reduce_copies(self, m, c, phase):
        axis = ORDER[c][phase]
        p, left, right = self.at[axis], self.left[axis], self.right[axis]
        one, of_left, of_right = (b.at[m, c] for b in self.bufs[phase])
        after, before, across = (p + 1) % 4, (p + 3) % 4, (p + 2) % 4
        block = functools.partial(self.block, m, c, phase)
        parts = (
            (block(0, across), one.at[0], right),
            (block(1, across), one.at[1], left),
            (block(1, after), of_left.at[1], right),
            (block(0, before), of_right.at[0], left),
            (one.at[0], of_left.at[0], right),
            (one.at[1], of_right.at[1], left),
        )
        return [functools.partial(self.copy, (m, c, phase, i), *part) for i, part in enumerate(parts)]

    def own_copies(self, m, c):
        p = self.at[ORDER[c][0]]
        blocks = ((0, (p + 1) % 4), (1, (p + 3) % 4), (0, p), (1, p))
        return [
            functools.partial(pltpu.make_async_copy, self.block(m, c, 0, *b), self.own.at[m, c, i], self.own_sem.at[3 * m + c, i])
            for i, b in enumerate(blocks)
        ]

    def add(self, phase, into, *others):
        def total(where):
            t = into[where].astype(F32)
            for o in others:
                t += o[where].astype(F32)
            into[where] = t.astype(BF16)

        if phase == 2:
            total(Ellipsis)
        elif phase == 1:
            for i in range(4):
                total((i,))
        else:

            def some(i, _):
                for k in range(4):
                    total((i, k))
                return 0

            lax.fori_loop(0, 4, some, 0)

    def begin(self, m, c, phase):
        for copy in self.reduce_copies(m, c, phase)[:4]:
            copy().start()
        if phase == 0:
            for copy in self.own_copies(m, c):
                copy().start()

    def pass_on(self, m, c, phase):
        copies = self.reduce_copies(m, c, phase)
        p = self.at[ORDER[c][phase]]
        one = self.bufs[phase][0].at[m, c]
        mine = self.own_copies(m, c) if phase == 0 else None
        for half, k in ((0, (p + 1) % 4), (1, (p + 3) % 4)):
            if phase == 0:
                mine[half]().wait()
            copies[half]().wait_recv()
            self.add(phase, one.at[half], self.own.at[m, c, half] if phase == 0 else self.block(m, c, phase, half, k))
            copies[4 + half]().start()

    def finish(self, m, c, phase):
        copies = self.reduce_copies(m, c, phase)
        p = self.at[ORDER[c][phase]]
        _, of_left, of_right = (b.at[m, c] for b in self.bufs[phase])
        mine = self.own_copies(m, c) if phase == 0 else None
        for half in range(2):
            if phase == 0:
                mine[2 + half]().wait()
            here = self.own.at[m, c, 2 + half] if phase == 0 else self.block(m, c, phase, half, p)
            for i in ((4, 3), (2, 5))[half]:
                copies[i]().wait_recv()
            if phase < 2:
                self.add(phase, of_left.at[half], of_right.at[half], here)
            else:
                self.update(m, 2 * c + half, of_left[half].astype(F32) + of_right[half].astype(F32) + here[...].astype(F32))

    def update(self, m, j, g):
        g = g.astype(BF16).astype(F32)
        self.sum[m, j] = g
        x, y, z = self.at
        n = self.number
        if m == 0:
            where = (n, slice(None), pl.ds(128 * j, 128))
            new = adamw(self.w[m][where].astype(F32), self.m[m][where], self.v[m][where], g)[0]
        else:
            self.scratch[0] = g
            for q in range(4):
                rows = pl.ds(12 * q, 12)
                where = (n, slice(None), pl.ds(512 * j + 128 * q, 128))
                self.scratch[1, rows, :] = adamw(
                    self.w[m][where].astype(F32), self.m[m][where], self.v[m][where], self.scratch[0, rows, :]
                )[0]
            new = self.scratch[1]
        self.full[m, j, x, y, z] = new.astype(BF16)

    def spread(self, m, c, phase, halves, k):
        axis, done = ORDER[c][2 - phase], ORDER[c][3 - phase :]
        where = tuple(slice(None) if a in done else k if a == axis else self.at[a] for a in range(3))
        return self.full.at[(m, halves, *where)]

    def gather_copies(self, m, c, phase, arriving=False):
        axis = ORDER[c][2 - phase]
        p, left, right = self.at[axis], self.left[axis], self.right[axis]
        both, a, b = pl.ds(2 * c, 2), pl.ds(2 * c, 1), pl.ds(2 * c + 1, 1)
        after, before, across = (p + 1) % 4, (p + 3) % 4, (p + 2) % 4
        parts = ((both, p, right), (both, p, left), (a, before, right), (b, after, left))
        if arriving:
            parts = ((both, before, right), (both, after, left), (a, across, right), (b, across, left))
        copies = []
        for i, (halves, k, to) in enumerate(parts):
            here = self.spread(m, c, phase, halves, k)
            copies.append(functools.partial(self.copy, (m, c, 3 + phase, i), here, here, to))
        return copies

    def out_copy(self, m, c):
        both = pl.ds(2 * c, 2)
        return pltpu.make_async_copy(self.full.at[m, both], self.out.at[m, both], self.out_sem.at[3 * m + c])

    def event(self, m, n):
        for c in range(3):
            if n == 0:
                self.begin(m, c, 0)
            elif n <= 6:
                phase = (n - 1) // 2
                if n % 2:
                    self.pass_on(m, c, phase)
                else:
                    self.finish(m, c, phase)
                    if phase < 2:
                        self.begin(m, c, phase + 1)
                    else:
                        for copy in self.gather_copies(m, c, 0)[:2]:
                            copy().start()
            else:
                phase = (n - 7) // 2
                copies = self.gather_copies(m, c, phase)
                arriving = self.gather_copies(m, c, phase, arriving=True)
                if n % 2:
                    for i in range(2):
                        arriving[i]().wait_recv()
                        copies[2 + i]().start()
                else:
                    arriving[2]().wait_recv()
                    arriving[3]().wait_recv()
                    if phase < 2:
                        for copy in self.gather_copies(m, c, phase + 1)[:2]:
                            copy().start()
                    else:
                        self.out_copy(m, c).start()

    def end(self):
        for m in range(3):
            for c in range(3):
                for phase in range(3):
                    for copy in self.reduce_copies(m, c, phase):
                        copy().wait_send()
                    for copy in self.gather_copies(m, c, phase):
                        copy().wait_send()
                self.out_copy(m, c).wait()


EVENTS = 13


def staggered(lag):
    order = []
    for t in range(EVENTS + 2 * lag):
        order += [(m, t - lag * m) for m in range(3) if 0 <= t - lag * m < EVENTS]
    return order


def exchange_kernel(number, *refs):
    g, w, m, v = (refs[i : i + 3] for i in (0, 3, 6, 9))
    sums, out = refs[12:14]
    full, own, scratch = refs[14:17]
    bufs = [refs[17 + 3 * i : 20 + 3 * i] for i in range(3)]
    sems = refs[26:30]
    ex = Exchange(number, g, w, m, v, sums, full, out, bufs, own, scratch, sems)
    ex.barrier()
    for event in staggered(1):
        ex.event(*event)
    ex.end()


def exchange(number, g, w, m, v):
    shapes = [(3, 3, 2, 4, 4, 48, 128), (3, 3, 2, 4, 48, 128), (3, 3, 2, 48, 128)]
    return pl.pallas_call(
        functools.partial(exchange_kernel, number),
        in_specs=[ANY] * 3 + [VMEM] * 9,
        out_specs=[VMEM, ANY],
        out_shape=[jax.ShapeDtypeStruct((3, 6, 48, 128), F32), jax.ShapeDtypeStruct((3, 6, 4, 4, 4, 48, 128), BF16)],
        scratch_shapes=[
            pltpu.VMEM((3, 6, 4, 4, 4, 48, 128), BF16),
            pltpu.VMEM((3, 3, 4, 4, 4, 48, 128), BF16),
            pltpu.VMEM((2, 48, 128), F32),
            *[pltpu.VMEM(s, BF16) for s in shapes for _ in range(3)],
            pltpu.SemaphoreType.DMA((9, 36)),
            pltpu.SemaphoreType.DMA((9, 36)),
            pltpu.SemaphoreType.DMA((9, 4)),
            pltpu.SemaphoreType.DMA((9,)),
        ],
        compiler_params=pltpu.CompilerParams(collective_id=number, has_side_effects=True, vmem_limit_bytes=VMEM_LIMIT),
        name=f"exchange_{number}",
    )(*[t.reshape(6, 4, 4, 4, 48, 128) for t in g], *w, *m, *v)


def results_kernel(*refs):
    full, sums, m, v = refs[0:2], refs[2:4], refs[4:7], refs[7:10]
    new_w, new_m, new_v = refs[10:13], refs[13:16], refs[16:19]
    for n in range(2):
        for j in range(6):
            columns = pl.ds(128 * j, 128)
            new_w[0][n, :, columns] = full[n][0, j].reshape(192, 128)
            for k in (1, 2):
                block = full[n][k, j].astype(F32)
                for q in range(4):
                    rows = jnp.concatenate([block[z, 12 * q : 12 * q + 12] for z in range(4)], axis=0)
                    new_w[k][n, :, pl.ds(512 * j + 128 * q, 128)] = rows.astype(BF16)

    @pl.when(pl.program_id(0) == 0)
    def _():
        for n in range(2):
            for j in range(6):
                for k in range(3):
                    for q in range(4 if k else 1):
                        g = sums[n][k, j, 12 * q : 12 * q + 12, :] if k else sums[n][k, j]
                        where = (n, slice(None), pl.ds(512 * j + 128 * q if k else 128 * j, 128))
                        new_m[k][where] = 0.9 * m[k][where] + 0.1 * g
                        new_v[k][where] = 0.95 * v[k][where] + 0.05 * g * g


def results(full, sums, m, v):
    def whole(t):
        return pl.BlockSpec(t.shape, lambda i: (0,) * t.ndim)

    full = [t.reshape(3, 6, 64, 48, 128) for t in full]
    part = pl.BlockSpec((3, 6, 4, 48, 128), lambda i: (0, 0, i, 0, 0))
    shapes = [(2, 3072, 768), (2, 768, 3072), (2, 768, 3072)]
    return pl.pallas_call(
        results_kernel,
        grid=(16,),
        in_specs=[part] * 2 + [whole(t) for t in (*sums, *m, *v)],
        out_specs=[pl.BlockSpec((2, s[1] // 16, s[2]), lambda i: (0, i, 0)) for s in shapes] + [whole(t) for t in (*m, *v)],
        out_shape=[jax.ShapeDtypeStruct(s, BF16) for s in shapes] + [jax.ShapeDtypeStruct(t.shape, F32) for t in (*m, *v)],
        compiler_params=pltpu.CompilerParams(vmem_limit_bytes=VMEM_LIMIT),
        name="results",
    )(*full, *sums, *m, *v)


def scale_of(wide):
    return lax.rsqrt(jnp.mean(wide**2, -1, keepdims=True) + 1e-6)


def normed(h):
    wide = h.astype(F32)
    return (wide * scale_of(wide)).astype(BF16)


def normed_back(h, d):
    wide, d = h.astype(F32), d.astype(F32)
    scale = scale_of(wide)
    return (scale * d - wide * (scale**3 * jnp.mean(wide * d, -1, keepdims=True))).astype(BF16)


def wide_of(a, w_gate, w_up):
    return jnp.dot(a, w_gate, preferred_element_type=F32), jnp.dot(a, w_up, preferred_element_type=F32)


def back_of_gate(gate, up, d):
    d = d.astype(F32)
    sig = jax.nn.sigmoid(gate)
    silu = gate * sig
    return (d * up * (sig + silu * (1 - sig))).astype(BF16), (d * silu).astype(BF16)


def solution(mesh):
    def step(x, dy, w_gate, w_up, w_down, m_gate, m_up, m_down, v_gate, v_up, v_down):
        h0, dy = x[0], dy[0]
        me = lax.axis_index("dp")
        w = (w_down, w_gate, w_up)
        m, v = (m_down, m_gate, m_up), (v_down, v_gate, v_up)
        mine = [lax.dynamic_slice_in_dim(t, me * (t.shape[1] // 64), t.shape[1] // 64, 1) for t in w]

        a0 = normed(h0)
        gate0, up0 = wide_of(a0, w_gate[0], w_up[0])
        act0 = (jax.nn.silu(gate0) * up0).astype(BF16)
        h1 = h0 + matmul(act0, w_down[0])
        a1 = normed(h1)
        gate1, up1 = wide_of(a1, w_gate[1], w_up[1])
        act1 = (jax.nn.silu(gate1) * up1).astype(BF16)

        d_gate, d_up = back_of_gate(gate1, up1, matmul(dy, w_down[1].T))
        g1 = [down_gradient(act1, dy), wide_gradient(a1, d_gate), wide_gradient(a1, d_up)]
        d_a = matmul(d_gate, w_gate[1].T) + matmul(d_up, w_up[1].T)
        d_h = dy + normed_back(h1, d_a)
        sums1, full1 = exchange(1, g1, mine, m, v)

        d_gate, d_up = back_of_gate(gate0, up0, matmul(d_h, w_down[0].T))
        g0 = [down_gradient(act0, d_h), wide_gradient(a0, d_gate), wide_gradient(a0, d_up)]
        sums0, full0 = exchange(0, g0, mine, m, v)

        new = results((full0, full1), (sums0, sums1), m, v)
        return tuple(new[3 * i + k] for i in range(3) for k in (1, 2, 0))

    rows = P(None, "dp", None)
    return jax.shard_map(
        step,
        mesh=mesh,
        in_specs=(P(("rep", "dp")),) * 2 + (P(),) * 3 + (rows,) * 6,
        out_specs=(P("rep"),) * 3 + (P("rep", "dp"),) * 6,
        check_vma=False,
    )
```

time: 1500 us -> 586 us (0.39)
  blocking collectives: 565 us -> 0 us
  Pallas kernels: 0 us -> 367 us
  waiting for transfers between devices: 214 us -> 0 us
  local copies, waits for them, and re-layouts: 202 us -> 16.3 us
  starting transfers between devices: 172 us -> 0 us
  matrix products: 262 us -> 184 us
  other arithmetic: 53.8 us -> 8.27 us
  between operations: 17.8 us -> 1.31 us
    unnamed x1 -> x0, blocking collectives: 565 us -> none
    pallas_call x0 -> x9, Pallas kernels: none -> 367 us  [the longest x2 246 us: exchange(): pl.pallas_call(functools.partial(exchange_kernel, number), in_specs=[ANY]...]
    reshape x3 -> x0, waiting for transfers between devices: 213 us -> none  [step(): t.reshape(-1, *t.shape[2:])]
    unnamed x174 -> x42, local copies, waits for them, and re-layouts: 198 us -> 12.8 us
    unnamed x66 -> x0, starting transfers between devices: 171 us -> none
    dot_general x15 -> x9, matrix products: 262 us -> 184 us  [the longest x5 91.7 us: matmul(): return jnp.dot(a, w, preferred_element_type=F32).astype(BF16)]
    unnamed x7 -> x0, other arithmetic: 45.2 us -> none
  transfers between devices with their start and end apart: 69 -> 0, of which waited for: 3 -> 0; matrix products, arithmetic and copies ran while one was open for 59% -> 0% of each run, Pallas kernels for 0% -> 0%
where the time goes in v1:
time: 586 us; the launch traced here: 577 us
  Pallas kernels  367 us (63%)
  matrix products  184 us (31%)
  local copies, waits for them, and re-layouts  16.3 us (3%)
  other arithmetic  8.27 us (1%)
    pallas_call x2, Pallas kernels, exchange(): pl.pallas_call(functools.partial(exchange_kernel, number), in_specs=[ANY]...  246 us
    dot_general x5, matrix products, matmul(): return jnp.dot(a, w, preferred_element_type=F32).astype(BF16)  91.7 us
    pallas_call x4, Pallas kernels, wide_gradient(): pl.pallas_call(wide_kernel, grid=(6,), in_specs=[pl.BlockSpec((tokens, ro...  64.4 us
    dot_general x2, matrix products, wide_of(): jnp.dot(a, w_up, preferred_element_type=F32)  57.5 us
    dot_general x2, matrix products, wide_of(): jnp.dot(a, w_gate, preferred_element_type=F32)  35.1 us
    pallas_call x2, Pallas kernels, down_gradient(): pl.pallas_call(down_kernel, grid=(6,), in_specs=[pl.BlockSpec((tokens, 51...  29.7 us
    pallas_call x1, Pallas kernels, results(): pl.pallas_call(results_kernel, grid=(16,), in_specs=[part] * 2 + [whole(t...  27 us
    unnamed x42, local copies, waits for them, and re-layouts  12.8 us

profile of v1, /device:TPU:0, one launch (start us, length us, event | category | flops | bytes accessed | tf_op | source)
XLA Modules:
  0.0 577.1 jit_solution(2349973517553050592)
XLA Ops:
  0.6 2.6 fusion.8
  3.2 0.0 copy-start.13
  3.2 0.0 copy-start
  3.3 17.7 %fusion.29 = f32[2048,3072]{1,0:T(8,128)} fusion(bf16[2,768,3072]{2,1,0:T(8,128)(2,1)} %param.13, bf16[1,2048,768]{2,1,0:T(8,128)(2,1)} %param.11, f32[2048]{0:T(1024)S(1)} %add_rsqrt_fusion.1), kind=kOutput, calls=%fused_computation.47 | convolution fusion | flops 9668395008 | bytes 33038336 | tf_op jit(solution)/shard_map/dot_general | solution.py:388
  20.9 0.0 copy-done.13
  20.9 0.0 copy-done
  20.9 24.7 %multiply_convert_fusion.1 = (bf16[2048,3072]{1,0:T(8,128)(2,1)}, f32[2048,3072]{1,0:T(8,128)}) fusion(f32[2048,3072]{1,0:T(8,128)} %fusion.29, bf16[2,768,3072]{2,1,0:T(8,128)(2,1)} %param.14, bf16[1,2048,768]{2,1,0:T(8,128)(2,1)S(1)} %copy-done, f32[2048]{0:T(1024)S(1)} %add_rsqrt_fusion.1), kind=kOutput, calls=%fused_computation.12 | convolution fusion | flops 9706143744 | bytes 70787072 | tf_op jit(solution)/shard_map/dot_general | solution.py:388
  45.6 14.5 %fusion.12 = (f32[2048]{0:T(1024)S(1)}, bf16[2048,768]{1,0:T(8,128)(2,1)S(1)}) fusion(bf16[2048,3072]{1,0:T(8,128)(2,1)} %get-tuple-element.49.act_ref, bf16[2,3072,768]{2,1,0:T(8,128)(2,1)} %param.15, bf16[1,2048,768]{2,1,0:T(8,128)(2,1)S(1)} %copy-done), kind=kOutput, calls=%fused_computation.29 | convolution fusion | flops 9671538688 | bytes 23601152 | tf_op jit(solution)/shard_map/dot_general | solution.py:21
  60.1 0.0 copy-start.2
  60.1 0.0 copy-start.15
  60.1 0.0 copy-start.11
  60.2 1.6 copy-done.2
  61.7 0.0 copy-done.15
  61.7 0.0 copy-done.11
  61.7 0.6 fusion.13.a_ref
  62.3 0.0 copy-start.4
  62.3 0.0 copy-start.5
  62.3 17.4 %fusion.17 = f32[2048,3072]{1,0:T(8,128)} fusion(bf16[2048,768]{1,0:T(8,128)(2,1)S(1)} %fusion.13.a_ref, bf16[2,768,3072]{2,1,0:T(8,128)(2,1)} %param.13), kind=kOutput, calls=%fused_computation.35 | convolution fusion | flops 9663676416 | bytes 33030144 | tf_op jit(solution)/shard_map/dot_general | solution.py:388
  79.7 0.0 copy-done.5
  79.7 14.8 %convolution_convert_fusion.1 = bf16[2048,3072]{1,0:T(8,128)(2,1)} fusion(bf16[2,3072,768]{2,1,0:T(8,128)(2,1)} %param.15, bf16[1,2048,768]{2,1,0:T(8,128)(2,1)S(1)} %copy-done.5), kind=kOutput, calls=%fused_computation.17 | convolution fusion | flops 9669967872 | bytes 20447232 | tf_op jit(solution)/shard_map/dot_general | solution.py:21
  94.6 0.0 copy-done.4
  94.6 32.8 %multiply_convert_fusion = (bf16[2048,3072]{1,0:T(8,128)(2,1)}, bf16[2048,3072]{1,0:T(8,128)(2,1)}, bf16[2048,3072]{1,0:T(8,128)(2,1)}) fusion(f32[2048,3072]{1,0:T(8,128)} %fusion.17, bf16[2048,3072]{1,0:T(8,128)(2,1)} %convolution_convert_fusion.1, bf16[2048,768]{1,0:T(8,128)(2,1)S(1)} %fusion.13.a_ref, bf16[2,768,3072]{2,1,0:T(8,128)(2,1)} %param.14), kind=kOutput, calls=%fused_computation.10 | convolution fusion | flops 9758048256 | bytes 83361792 | tf_op jit(solution)/shard_map/dot_general | solution.py:388
  127.4 16.1 %shard_map.182 = bf16[6,64,48,128]{3,2,1,0:T(8,128)(2,1)} custom-call(bf16[2048,768]{1,0:T(8,128)(2,1)} %copy-done.4, bf16[2048,3072]{1,0:T(8,128)(2,1)} %get-tuple-element.45.d_ref), custom_call_target="tpu_custom_call" | custom-call | flops 9663676416 | bytes 20971520 | tf_op jit(solution)/shard_map/pallas_call | solution.py:43
  143.5 16.1 %shard_map.183 = bf16[6,64,48,128]{3,2,1,0:T(8,128)(2,1)} custom-call(bf16[2048,768]{1,0:T(8,128)(2,1)} %copy-done.4, bf16[2048,3072]{1,0:T(8,128)(2,1)} %get-tuple-element.46.d_ref), custom_call_target="tpu_custom_call" | custom-call | flops 9663676416 | bytes 20971520 | tf_op jit(solution)/shard_map/pallas_call | solution.py:43
  159.5 0.0 copy-start.7
  159.6 0.0 copy-start.8
  159.6 0.0 copy-start.9
  159.6 0.0 copy-start.10
  159.6 14.9 %shard_map.181 = bf16[6,3072,128]{2,1,0:T(8,128)(2,1)} custom-call(bf16[2048,3072]{1,0:T(8,128)(2,1)} %get-tuple-element.44.act_ref, bf16[2048,768]{1,0:T(8,128)(2,1)} %bitcast.80), custom_call_target="tpu_custom_call" | custom-call | flops 9663676416 | bytes 20971520 | tf_op jit(solution)/shard_map/pallas_call | solution.py:63
  174.4 1.9 constant_dynamic-slice_fusion
  176.3 1.6 constant_dynamic-slice_fusion.2.refs_3_
  177.9 0.0 copy-done.7
  177.9 0.9 copy.23.refs_7_.refs_5_
  178.8 0.0 copy-done.8
  178.8 0.9 copy.24.refs_8_.refs_6_
  179.6 0.0 copy-done.9
  179.6 0.9 copy.25.refs_10_.refs_8_
  180.5 0.0 copy-done.10
  180.5 0.8 copy.26.refs_11_.refs_9_
  181.3 128.1 %exchange_1.1 = (f32[3,6,48,128]{3,2,1,0:T(8,128)}, bf16[3,6,4,4,4,48,128]{6,5,4,3,2,1,0:T(8,128)(2,1)}) custom-call(bf16[6,4,4,4,48,128]{5,4,3,2,1,0:T(8,128)(2,1)} %bitcast.76, bf16[6,4,4,4,48,128]{5,4,3,2,1,0:T(8,128)(2,1)} %bitcast.74, bf16[6,4,4,4,48,128]{5,4,3,2,1,0:T(8,128)(2,1)} %bitcast.75, ...), custom_call_target="tpu_custom_call" | custom-call | tf_op jit(solution)/shard_map/exchange_1/pallas_call | solution.py:309
  309.4 0.0 copy-start.3
  309.4 14.5 %fusion.43 = bf16[2048,768]{1,0:T(8,128)(2,1)S(1)} fusion(bf16[2048,3072]{1,0:T(8,128)(2,1)} %get-tuple-element.46.d_ref, bf16[2,768,3072]{2,1,0:T(8,128)(2,1)} %param.14), kind=kOutput, calls=%fused_computation.59 | convolution fusion | flops 9665249280 | bytes 20447232 | tf_op jit(solution)/shard_map/dot_general | solution.py:21
  323.9 0.0 copy-done.3
  323.9 0.0 copy-start.16
  323.9 0.0 copy-start.6
  323.9 0.0 copy-start.12
  323.9 15.1 %fusion.14 = (f32[2048]{0:T(1024)S(1)}, bf16[2048,768]{1,0:T(8,128)(2,1)S(1)}) fusion(bf16[2048,768]{1,0:T(8,128)(2,1)S(1)} %copy-done.3, bf16[2048,768]{1,0:T(8,128)(2,1)S(1)} %fusion.43, bf16[2048,3072]{1,0:T(8,128)(2,1)} %get-tuple-element.45.d_ref, bf16[2,768,3072]{2,1,0:T(8,128)(2,1)} %param.13), kind=kOutput, calls=%fused_computation.31 | convolution fusion | flops 9673111552 | bytes 26746880 | tf_op jit(solution)/shard_map/dot_general | solution.py:21
  339.1 0.0 copy-done.16
  339.1 0.0 copy-done.6
  339.1 0.0 copy-done.12
  339.1 2.9 fusion.50.d_ref
  342.0 32.9 %fusion.5 = (bf16[2048,3072]{1,0:T(8,128)(2,1)}, bf16[2048,3072]{1,0:T(8,128)(2,1)}) fusion(f32[2048,3072]{1,0:T(8,128)} %fusion.29, f32[2048,3072]{1,0:T(8,128)} %get-tuple-element.50, bf16[2048,768]{1,0:T(8,128)(2,1)} %fusion.50.d_ref, bf16[2,3072,768]{2,1,0:T(8,128)(2,1)} %param.15), kind=kOutput, calls=%fused_computation.9 | convolution fusion | flops 9751756800 | bytes 83361792 | tf_op jit(solution)/shard_map/dot_general | solution.py:21
  374.8 0.0 copy-done.1
  374.8 0.0 copy-done.14
  374.8 2.2 fusion.9.a_ref
  377.1 16.1 %shard_map.180 = bf16[6,64,48,128]{3,2,1,0:T(8,128)(2,1)} custom-call(bf16[2048,768]{1,0:T(8,128)(2,1)} %fusion.9.a_ref, bf16[2048,3072]{1,0:T(8,128)(2,1)} %get-tuple-element.47.d_ref), custom_call_target="tpu_custom_call" | custom-call | flops 9663676416 | bytes 20971520 | tf_op jit(solution)/shard_map/pallas_call | solution.py:43
  393.2 16.1 %shard_map.179 = bf16[6,64,48,128]{3,2,1,0:T(8,128)(2,1)} custom-call(bf16[2048,768]{1,0:T(8,128)(2,1)} %fusion.9.a_ref, bf16[2048,3072]{1,0:T(8,128)(2,1)} %get-tuple-element.48.d_ref), custom_call_target="tpu_custom_call" | custom-call | flops 9663676416 | bytes 20971520 | tf_op jit(solution)/shard_map/pallas_call | solution.py:43
  409.3 14.8 %shard_map.178 = bf16[6,3072,128]{2,1,0:T(8,128)(2,1)} custom-call(bf16[2048,3072]{1,0:T(8,128)(2,1)} %get-tuple-element.49.act_ref, bf16[2048,768]{1,0:T(8,128)(2,1)} %fusion.50.d_ref), custom_call_target="tpu_custom_call" | custom-call | flops 9663676416 | bytes 20971520 | tf_op jit(solution)/shard_map/pallas_call | solution.py:63
  424.1 117.8 %exchange_0.1 = (f32[3,6,48,128]{3,2,1,0:T(8,128)}, bf16[3,6,4,4,4,48,128]{6,5,4,3,2,1,0:T(8,128)(2,1)}) custom-call(bf16[6,4,4,4,48,128]{5,4,3,2,1,0:T(8,128)(2,1)} %bitcast.79, bf16[6,4,4,4,48,128]{5,4,3,2,1,0:T(8,128)(2,1)} %bitcast.78, bf16[6,4,4,4,48,128]{5,4,3,2,1,0:T(8,128)(2,1)} %bitcast.77, ...), custom_call_target="tpu_custom_call" | custom-call | tf_op jit(solution)/shard_map/exchange_0/pallas_call | solution.py:309
  542.0 27.0 %results.1 = (bf16[2,3072,768]{2,1,0:T(8,128)(2,1)}, bf16[2,768,3072]{2,1,0:T(8,128)(2,1)}, bf16[2,768,3072]{2,1,0:T(8,128)(2,1)}, f32[2,48,768]{2,1,0:T(8,128)}...) custom-call(bf16[3,6,64,48,128]{4,3,2,1,0:T(8,128)(2,1)} %bitcast.73, ...), custom_call_target="tpu_custom_call" | custom-call | tf_op jit(solution)/shard_map/results/pallas_call | solution.py:361
  568.9 1.9 copy.35
  570.9 1.9 copy.36
  572.8 1.9 copy.37
  574.7 1.9 copy.38
  (5 shorter events, 0.0 us)
Async XLA Ops:
  3.2 17.7 %copy-start.13 = (f32[2048]{0:T(1024)}, f32[2048]{0:T(1024)S(1)}, u32[]{:S(2)}) copy-start(f32[2048]{0:T(1024)S(1)} %add_rsqrt_fusion.1) | copy-start | bytes 24580
  3.2 17.7 %copy-start = (bf16[1,2048,768]{2,1,0:T(8,128)(2,1)S(1)}, bf16[1,2048,768]{2,1,0:T(8,128)(2,1)}, u32[]{:S(2)}) copy-start(bf16[1,2048,768]{2,1,0:T(8,128)(2,1)} %param.11) | copy-start | bytes 9437188
  60.1 1.6 copy-start.2
  60.1 1.6 copy-start.15
  60.1 1.6 copy-start.11
  62.3 32.2 %copy-start.4 = (bf16[2048,768]{1,0:T(8,128)(2,1)}, bf16[2048,768]{1,0:T(8,128)(2,1)S(1)}, u32[]{:S(2)}) copy-start(bf16[2048,768]{1,0:T(8,128)(2,1)S(1)} %fusion.13.a_ref) | copy-start | bytes 9437188
  62.3 17.4 %copy-start.5 = (bf16[1,2048,768]{2,1,0:T(8,128)(2,1)S(1)}, bf16[1,2048,768]{2,1,0:T(8,128)(2,1)}, u32[]{:S(2)}) copy-start(bf16[1,2048,768]{2,1,0:T(8,128)(2,1)} %param.12) | copy-start | bytes 9437188
  159.5 18.4 %copy-start.7 = (f32[2,12,3072]{2,0,1:T(2,128)S(1)}, f32[2,12,3072]{2,0,1:T(2,128)}, u32[]{:S(2)}) copy-start(f32[2,12,3072]{2,0,1:T(2,128)} %param.16) | copy-start | bytes 884740
  159.6 19.2 %copy-start.8 = (f32[2,12,3072]{2,0,1:T(2,128)S(1)}, f32[2,12,3072]{2,0,1:T(2,128)}, u32[]{:S(2)}) copy-start(f32[2,12,3072]{2,0,1:T(2,128)} %param.17) | copy-start | bytes 884740
  159.6 20.1 %copy-start.9 = (f32[2,12,3072]{2,0,1:T(2,128)S(1)}, f32[2,12,3072]{2,0,1:T(2,128)}, u32[]{:S(2)}) copy-start(f32[2,12,3072]{2,0,1:T(2,128)} %param.19) | copy-start | bytes 884740
  159.6 20.9 %copy-start.10 = (f32[2,12,3072]{2,0,1:T(2,128)S(1)}, f32[2,12,3072]{2,0,1:T(2,128)}, u32[]{:S(2)}) copy-start(f32[2,12,3072]{2,0,1:T(2,128)} %param.20) | copy-start | bytes 884740
  309.4 14.5 %copy-start.3 = (bf16[2048,768]{1,0:T(8,128)(2,1)S(1)}, bf16[2048,768]{1,0:T(8,128)(2,1)}, u32[]{:S(2)}) copy-start(bf16[2048,768]{1,0:T(8,128)(2,1)} %copy-done.2) | copy-start | bytes 9437188
  323.9 15.2 %copy-start.16 = (f32[2048]{0:T(1024)S(1)}, f32[2048]{0:T(1024)}, u32[]{:S(2)}) copy-start(f32[2048]{0:T(1024)} %copy-done.15) | copy-start | bytes 24580
  323.9 15.2 %copy-start.6 = (bf16[1,2048,768]{2,1,0:T(8,128)(2,1)S(1)}, bf16[1,2048,768]{2,1,0:T(8,128)(2,1)}, u32[]{:S(2)}) copy-start(bf16[1,2048,768]{2,1,0:T(8,128)(2,1)} %param.12) | copy-start | bytes 9437188
  323.9 15.2 %copy-start.12 = (f32[2048]{0:T(1024)S(1)}, f32[2048]{0:T(1024)}, u32[]{:S(2)}) copy-start(f32[2048]{0:T(1024)} %copy-done.11) | copy-start | bytes 24580
  342.0 32.9 %copy-start.1 = (bf16[1,2048,768]{2,1,0:T(8,128)(2,1)S(1)}, bf16[1,2048,768]{2,1,0:T(8,128)(2,1)}, u32[]{:S(2)}) copy-start(bf16[1,2048,768]{2,1,0:T(8,128)(2,1)} %param.11) | copy-start | bytes 9437188
  342.0 32.9 %copy-start.14 = (f32[2048]{0:T(1024)S(1)}, f32[2048]{0:T(1024)}, u32[]{:S(2)}) copy-start(f32[2048]{0:T(1024)} %copy-done.13) | copy-start | bytes 24580

commit v2 on v1

v2 whole, which is shorter than its diff:
```python
import functools

import jax
import jax.numpy as jnp
from jax import lax
from jax.experimental import pallas as pl
from jax.experimental.pallas import tpu as pltpu
from jax.sharding import PartitionSpec as P

F32 = jnp.float32
BF16 = jnp.bfloat16
MESH = pl.DeviceIdType.MESH
ANY = pl.BlockSpec(memory_space=pl.ANY)
VMEM = pl.BlockSpec(memory_space=pltpu.VMEM)
STRIDE = (16, 4, 1)
ORDER = ((0, 1, 2), (1, 2, 0), (2, 0, 1))
VMEM_LIMIT = 60 * 1024 * 1024
ALL_VMEM = 67_043_328


def matmul(a, w):
    return jnp.dot(a, w, preferred_element_type=F32).astype(BF16)


def over_tokens(a, b):
    return lax.dot_general(a, b, (((0,), (0,)), ((), ())), preferred_element_type=F32)


def over_columns(a, b):
    return lax.dot_general(a, b, (((1,), (1,)), ((), ())), preferred_element_type=F32)


def scale_of(wide):
    return lax.rsqrt(jnp.mean(wide**2, -1, keepdims=True) + 1e-6)


def normed(h):
    wide = h.astype(F32)
    return (wide * scale_of(wide)).astype(BF16)


def normed_back(h, d):
    wide, d = h.astype(F32), d.astype(F32)
    scale = scale_of(wide)
    return (scale * d - wide * (scale**3 * jnp.mean(wide * d, -1, keepdims=True))).astype(BF16)


def adamw(w, m, v, g):
    m = 0.9 * m + 0.1 * g
    v = 0.95 * v + 0.05 * g * g
    step = m * lax.rsqrt(v + 1e-8) + 0.1 * w
    return w - 0.02 * step, m, v


def split(d):
    return lax.div(d, 16), lax.rem(lax.div(d, 4), 4), lax.rem(d, 4)


def axes(m, c):
    return ORDER[(m + c) % 3]


class Exchange:
    def __init__(self, layer, place, refs):
        self.layer = layer
        self.at, self.after, self.across, self.before, self.right, self.left = place
        self.g, self.w, self.m, self.v, self.sum, self.full, self.new, self.bufs, self.own, self.scratch = refs[:10]
        self.send_sem, self.recv_sem, self.own_sem, self.new_sem = refs[10:]

    def sem(self, m, c):
        return 3 * m + c

    def copy(self, m, c, n, src, dst, to):
        return pltpu.make_async_remote_copy(
            src_ref=src,
            dst_ref=dst,
            send_sem=self.send_sem.at[self.sem(m, c), n],
            recv_sem=self.recv_sem.at[self.sem(m, c), n],
            device_id={"dp": to},
            device_id_type=MESH,
        )

    def block(self, m, c, phase, half, k):
        axis = axes(m, c)[phase]
        place = sorted(axes(m, c)[phase:]).index(axis)
        where = (slice(None),) * place + (k,)
        if phase == 0:
            return self.g.at[(3 * self.layer + m, 2 * c + half, *where)]
        return self.bufs[phase - 1][1].at[(m, c, half, *where)]

    def reduce_copies(self, m, c, phase):
        axis = axes(m, c)[phase]
        p, left, right = self.at[axis], self.left[axis], self.right[axis]
        one, of_left, of_right = (b.at[m, c] for b in self.bufs[phase])
        after, before, across = self.after[axis], self.before[axis], self.across[axis]
        block = functools.partial(self.block, m, c, phase)
        parts = (
            (block(0, across), one.at[0], right),
            (block(1, across), one.at[1], left),
            (block(1, after), of_left.at[1], right),
            (block(0, before), of_right.at[0], left),
            (one.at[0], of_left.at[0], right),
            (one.at[1], of_right.at[1], left),
        )
        return [functools.partial(self.copy, m, c, 6 * phase + i, *part) for i, part in enumerate(parts)]

    def own_copies(self, m, c):
        axis = axes(m, c)[0]
        p = self.at[axis]
        blocks = ((0, self.after[axis]), (1, self.before[axis]), (0, p), (1, p))
        return [
            functools.partial(pltpu.make_async_copy, self.block(m, c, 0, *b), self.own.at[m, c, i % 2], self.own_sem.at[3 * m + c, i % 2])
            for i, b in enumerate(blocks)
        ]

    def add(self, phase, into, *others):
        def total(where):
            t = into[where].astype(F32)
            for o in others:
                t += o[where].astype(F32)
            into[where] = t.astype(BF16)

        if phase == 2:
            total(Ellipsis)
        elif phase == 1:
            for i in range(4):
                total((i,))
        else:

            def some(i, _):
                for k in range(4):
                    total((i, k))
                return 0

            lax.fori_loop(0, 4, some, 0)

    def begin(self, m, c, phase):
        for copy in self.reduce_copies(m, c, phase)[:4]:
            copy().start()
        if phase == 0:
            for copy in self.own_copies(m, c)[:2]:
                copy().start()

    def pass_on(self, m, c, phase):
        copies = self.reduce_copies(m, c, phase)
        axis = axes(m, c)[phase]
        one = self.bufs[phase][0].at[m, c]
        mine = self.own_copies(m, c) if phase == 0 else None
        for half, k in ((0, self.after[axis]), (1, self.before[axis])):
            if phase == 0:
                mine[half]().wait()
            copies[half]().wait_recv()
            self.add(phase, one.at[half], self.own.at[m, c, half] if phase == 0 else self.block(m, c, phase, half, k))
            copies[4 + half]().start()
            if phase == 0:
                mine[2 + half]().start()

    def finish(self, m, c, phase):
        copies = self.reduce_copies(m, c, phase)
        p = self.at[axes(m, c)[phase]]
        _, of_left, of_right = (b.at[m, c] for b in self.bufs[phase])
        mine = self.own_copies(m, c) if phase == 0 else None
        for half in range(2):
            if phase == 0:
                mine[2 + half]().wait()
            here = self.own.at[m, c, half] if phase == 0 else self.block(m, c, phase, half, p)
            for i in ((4, 3), (2, 5))[half]:
                copies[i]().wait_recv()
            if phase < 2:
                self.add(phase, of_left.at[half], of_right.at[half], here)
            else:
                self.update(m, 2 * c + half, of_left[half].astype(F32) + of_right[half].astype(F32) + here[...].astype(F32))

    def update(self, m, j, g):
        g = g.astype(BF16).astype(F32)
        n = self.layer
        self.sum[m, j] = g
        if m == 0:
            where = (n, slice(None), pl.ds(128 * j, 128))
            new = adamw(self.w[m][where].astype(F32), self.m[m][where], self.v[m][where], g)[0]
        else:
            self.scratch[0] = g
            for q in range(4):
                rows = pl.ds(12 * q, 12)
                where = (n, slice(None), pl.ds(512 * j + 128 * q, 128))
                self.scratch[1, rows, :] = adamw(
                    self.w[m][where].astype(F32), self.m[m][where], self.v[m][where], self.scratch[0, rows, :]
                )[0]
            new = self.scratch[1]
        self.new[m, j] = new.astype(BF16)

    def spread(self, m, c, phase, halves, k):
        axis, done = axes(m, c)[2 - phase], axes(m, c)[3 - phase :]
        where = tuple(slice(None) if a in done else k if a == axis else self.at[a] for a in range(3))
        return self.full.at[(m, halves, *where)]

    def gather_copies(self, m, c, phase, arriving=False):
        axis = axes(m, c)[2 - phase]
        p, left, right = self.at[axis], self.left[axis], self.right[axis]
        both, a, b = pl.ds(2 * c, 2), pl.ds(2 * c, 1), pl.ds(2 * c + 1, 1)
        after, before, across = self.after[axis], self.before[axis], self.across[axis]
        parts = ((both, p, right), (both, p, left), (a, before, right), (b, after, left))
        if arriving:
            parts = ((both, before, right), (both, after, left), (a, across, right), (b, across, left))
        copies = []
        for i, (halves, k, to) in enumerate(parts):
            here = self.spread(m, c, phase, halves, k)
            src = self.new.at[m, both] if phase == 0 and i < 2 else here
            copies.append(functools.partial(self.copy, m, c, 18 + 4 * phase + i, src, here, to))
        return copies

    def keep(self, m, c):
        x, y, z = self.at
        both = pl.ds(2 * c, 2)
        return pltpu.make_async_copy(
            self.new.at[m, both], self.full.at[m, both, x, y, z], self.new_sem.at[self.sem(m, c)]
        )

    def event(self, m, c, n):
        if n == 0:
            self.begin(m, c, 0)
        elif n <= 6:
            phase = (n - 1) // 2
            if n % 2:
                self.pass_on(m, c, phase)
            else:
                self.finish(m, c, phase)
                if phase < 2:
                    self.begin(m, c, phase + 1)
                else:
                    for copy in self.gather_copies(m, c, 0)[:2]:
                        copy().start()
                    self.keep(m, c).start()
        else:
            phase = (n - 7) // 2
            copies = self.gather_copies(m, c, phase)
            arriving = self.gather_copies(m, c, phase, arriving=True)
            if n % 2:
                for i in range(2):
                    arriving[i]().wait_recv()
                    copies[2 + i]().start()
            else:
                arriving[2]().wait_recv()
                arriving[3]().wait_recv()
                if n == 8:
                    self.keep(m, c).wait()
                if n == 10:
                    for i in range(3):
                        for copy in self.reduce_copies(m, c, i):
                            copy().wait_send()
                if phase < 2:
                    for copy in self.gather_copies(m, c, phase + 1)[:2]:
                        copy().start()

    def end(self):
        for m in range(3):
            for c in range(3):
                for phase in range(3):
                    for copy in self.gather_copies(m, c, phase):
                        copy().wait_send()


EVENTS = 13
UNITS, STEPS = 6, 7
TURN = UNITS * STEPS
LAST = 2 * TURN + 1
STEP_US = {1: (3.2,) * 4 + (2.7, 2.7, 2.5), 0: (2.2,) * 4 + (2.7, 2.7, 2.5)}
EVENT_US = (0.3, 0.8, 1.2, 0.3, 0.5, 0.2, 0.6, 0.2, 0.2, 0.2, 0.2, 0.2, 0.1)
HALF_US, HOP_US, SLACK_US = 4.3, 2.5, 1.0


def first_step(layer, m, c):
    if layer == 0:
        return 0
    return STEPS * (2 * c + 1) + 5 + m if m else TURN + 1


def schedule(layer, last):
    links = {}

    def send(time, axis, way, size):
        begin = max(time, links.get((axis, way), 0.0))
        links[axis, way] = begin + HALF_US * size
        return begin + HALF_US * size + HOP_US

    heads = {(layer, m, c): 0 for m in range(3) for c in range(3)}
    ready, forced = {}, {}
    order, now = [[] for _ in range(last + 1)], 0.0

    def run(key, time):
        layer, m, c = key
        n = heads[key]
        time += EVENT_US[n]
        heads[key] = n + 1
        arrival = time
        if n < 6:
            phase, size = n // 2, 0.25 ** (n // 2)
            axis = axes(m, c)[phase]
            if n % 2 == 0:
                forced[key] = 0.0
                for way in range(2):
                    arrival = max(arrival, send(time, axis, way, size))
                for way in range(2):
                    forced[key] = max(forced[key], send(time, axis, way, size))
            else:
                for way in range(2):
                    arrival = max(arrival, send(time, axis, way, size))
                arrival = max(arrival, forced[key])
        elif n < 12:
            phase, size = (n - 6) // 2, 0.25 ** (2 - (n - 6) // 2)
            axis = axes(m, c)[2 - phase]
            for way in range(2):
                arrival = max(arrival, send(time, axis, way, 2 * size if n % 2 == 0 else size))
        ready[key] = arrival
        return time

    for step in range(last + 1):
        while True:
            able = []
            for key, n in heads.items():
                if n == EVENTS:
                    continue
                if n == 0:
                    if step < first_step(*key):
                        continue
                    able.append((0.0, key))
                else:
                    able.append((ready[key] + SLACK_US, key))
            able.sort(key=lambda e: (e[0], -e[1][0], e[1][1:]))
            if not able or (step < last and able[0][0] > now):
                break
            time, key = able[0]
            order[step].append((*key, heads[key]))
            now = run(key, max(now, time))
        if step < last:
            now += 4.0 if step == TURN else STEP_US[1 if step < TURN else 0][(step - (step > TURN)) % STEPS]
    return order, now


def places():
    me = lax.axis_index("dp")
    at = split(me)
    after, across, before = (tuple(lax.rem(p + i, 4) for p in at) for i in (1, 2, 3))
    right, left = (tuple(me + STRIDE[i] * (to[i] - at[i]) for i in range(3)) for to in (after, before))
    return at, after, across, before, right, left


def greet(place):
    barrier = pltpu.get_barrier_semaphore()
    for axis in range(3):
        for to in (place[4][axis], place[5][axis]):
            pl.semaphore_signal(barrier, inc=1, device_id={"dp": to}, device_id_type=MESH)
    pl.semaphore_wait(barrier, 6)


def exchange_scratch():
    shapes = [(3, 3, 2, 4, 4, 48, 128), (3, 3, 2, 4, 48, 128), (3, 3, 2, 48, 128)]
    return [
        pltpu.VMEM((3, 3, 2, 4, 4, 48, 128), BF16),
        pltpu.VMEM((3, 6, 48, 128), BF16),
        pltpu.VMEM((2, 48, 128), F32),
        *[pltpu.VMEM(s, BF16) for s in shapes for _ in range(3)],
        pltpu.SemaphoreType.DMA((9, 30)),
        pltpu.SemaphoreType.DMA((9, 30)),
        pltpu.SemaphoreType.DMA((9, 2)),
        pltpu.SemaphoreType.DMA((9,)),
    ]


def exchange_of(layer, place, g, w, m, v, sums, full, scratch):
    own, new, small = scratch[:3]
    bufs = [scratch[3 + 3 * i : 6 + 3 * i] for i in range(3)]
    return Exchange(layer, place, (g, w, m, v, sums, full, new, bufs, own, small, *scratch[12:16]))


def exchange_kernel(*refs):
    g_ref = refs[0]
    w, m, v = refs[1:4], refs[4:7], refs[7:10]
    place = places()
    exchange = exchange_of(0, place, g_ref, w, m, v, *refs[10:12], refs[12:])
    greet(place)
    for _, m_, c, n in schedule(0, 0)[0][0]:
        exchange.event(m_, c, n)
    exchange.end()


EXCHANGED = [jax.ShapeDtypeStruct((3, 6, 48, 128), F32), jax.ShapeDtypeStruct((3, 6, 4, 4, 4, 48, 128), BF16)]


def exchange(g, w, m, v):
    return pl.pallas_call(
        exchange_kernel,
        in_specs=[ANY] + [VMEM] * 9,
        out_specs=[VMEM, ANY],
        out_shape=EXCHANGED,
        scratch_shapes=exchange_scratch(),
        compiler_params=pltpu.CompilerParams(collective_id=1, has_side_effects=True, vmem_limit_bytes=VMEM_LIMIT),
        name="exchange",
    )(g, *w, *m, *v)


def backward_kernel(*refs):
    a1_ref, a0_ref, h1_ref, dy_ref, w_gate_ref, w_up_ref, w_down_ref = refs[:7]
    w, m, v = refs[7:10], refs[10:13], refs[13:16]
    sum_ref, full_ref, g_ref = refs[16:19]
    a_ref, d_ref, da_ref, tile_ref, wg_ref, wu_ref, wd_ref, s_ref, wide_ref, down_ref, load_sem, weight_sem, store_sem = refs[19:32]
    place = places()
    exchange = exchange_of(1, place, g_ref, w, m, v, sum_ref, full_ref, refs[32:])

    def weights(unit):
        layer, j, slot = 1 - lax.div(unit, UNITS), lax.rem(unit, UNITS), lax.rem(unit, 2)
        some = pl.ds(pl.multiple_of(512 * j, 512), 512)
        return (
            pltpu.make_async_copy(w_gate_ref.at[layer, :, some], wg_ref.at[slot], weight_sem.at[slot, 0]),
            pltpu.make_async_copy(w_up_ref.at[layer, :, some], wu_ref.at[slot], weight_sem.at[slot, 1]),
            pltpu.make_async_copy(w_down_ref.at[layer, some, :], wd_ref.at[slot], weight_sem.at[slot, 2]),
        )

    def load(src, dst, i):
        return pltpu.make_async_copy(src, dst, load_sem.at[i])

    load(a1_ref, a_ref, 0).start()
    load(dy_ref, d_ref, 1).start()
    for copy in weights(jnp.int32(0)):
        copy.start()
    da_ref[...] = jnp.zeros_like(da_ref)
    load(a1_ref, a_ref, 0).wait()
    load(dy_ref, d_ref, 1).wait()
    greet(place)

    def tokens(layer, unit, block):
        rows = pl.ds(pl.multiple_of(512 * block, 512), 512)
        slot = lax.rem(unit, 2)
        a, d = a_ref[rows, :], d_ref[rows, :]
        gate = jnp.dot(a, wg_ref[slot], preferred_element_type=F32)
        up = jnp.dot(a, wu_ref[slot], preferred_element_type=F32)
        d_act = over_columns(d, wd_ref[slot]).astype(BF16).astype(F32)
        sig = jax.nn.sigmoid(gate)
        silu = gate * sig
        tile_ref[0, rows, :] = (silu * up).astype(BF16)
        d_gate = (d_act * up * (sig + silu * (1 - sig))).astype(BF16)
        d_up = (d_act * silu).astype(BF16)
        tile_ref[1, rows, :] = d_gate
        tile_ref[2, rows, :] = d_up

        @pl.when(layer == 1)
        def _():
            da_ref[rows, :] += over_columns(tile_ref[1, rows, :], wg_ref[slot]) + over_columns(tile_ref[2, rows, :], wu_ref[slot])

    def store_wide(layer, j, which):
        return pltpu.make_async_copy(wide_ref.at[which], g_ref.at[3 * layer + 1 + which, j], store_sem.at[which])

    def wide(layer, j, which):
        s_ref[...] = over_tokens(a_ref[...], tile_ref[1 + which])

        def two_devices(i, _):
            rows = s_ref[pl.ds(pl.multiple_of(24 * i, 8), 24), :]
            for k in range(2):
                block = [rows[12 * k : 12 * k + 12, 128 * q : 128 * q + 128] for q in range(4)]
                x, y, z = split(2 * i + k)
                wide_ref[which, x, y, z] = jnp.concatenate(block, axis=0).astype(BF16)
            return 0

        lax.fori_loop(0, 32, two_devices, 0)
        store_wide(layer, j, which).start()

        @pl.when(which == 1)
        def _():
            store_wide(layer, j, 0).wait()

    def store_down(layer):
        return pltpu.make_async_copy(down_ref, g_ref.at[3 * layer], store_sem.at[2])

    def down(layer, j):
        total = over_tokens(tile_ref[0], d_ref[...])
        for i in range(32):
            x, y, z = split(lax.div(32 * j + i, 3))
            rows = pl.ds(pl.multiple_of(16 * lax.rem(32 * j + i, 3), 16), 16)
            for k in range(6):
                down_ref[k, x, y, z, rows, :] = total[16 * i : 16 * i + 16, 128 * k : 128 * k + 128].astype(BF16)
        store_wide(layer, j, 1).wait()

        @pl.when(j == UNITS - 1)
        def _():
            store_down(layer).start()

    def turn():
        load(h1_ref, a_ref, 0).start()
        load(h1_ref, a_ref, 0).wait()

        def some(i, _):
            rows = pl.ds(pl.multiple_of(128 * i, 128), 128)
            back = normed_back(a_ref[rows, :], da_ref[rows, :].astype(BF16))
            d_ref[rows, :] = d_ref[rows, :] + back
            return 0

        lax.fori_loop(0, 16, some, 0)
        load(a0_ref, a_ref, 0).start()
        store_down(1).wait()
        load(a0_ref, a_ref, 0).wait()

    order, _ = schedule(1, LAST)

    def events(step, low, high):
        if not any(order[low:high]):
            return
        if high - low == 1:
            for _, m, c, n in order[low]:
                exchange.event(m, c, n)
            return
        middle = (low + high) // 2
        if any(order[low:middle]):
            pl.when(step < middle)(lambda: events(step, low, middle))
        if any(order[middle:high]):
            pl.when(step >= middle)(lambda: events(step, middle, high))

    def one_step(step, _):
        events(step, 0, LAST)
        turning = step == TURN
        at_work = jnp.where(step > TURN, step - 1, step)
        unit, kind = lax.div(at_work, STEPS), lax.rem(at_work, STEPS)
        layer, j = 1 - lax.div(unit, UNITS), lax.rem(unit, UNITS)
        working = jnp.logical_not(turning)

        @pl.when(jnp.logical_and(working, kind == 0))
        def _():
            for copy in weights(unit):
                copy.wait()

            @pl.when(unit < 2 * UNITS - 1)
            def _():
                for copy in weights(unit + 1):
                    copy.start()

        pl.when(jnp.logical_and(working, kind < 4))(lambda: tokens(layer, unit, kind))
        pl.when(jnp.logical_and(working, jnp.logical_or(kind == 4, kind == 5)))(lambda: wide(layer, j, kind - 4))
        pl.when(jnp.logical_and(working, kind == 6))(lambda: down(layer, j))
        pl.when(turning)(turn)
        return 0

    lax.fori_loop(0, LAST, one_step, 0)
    store_down(0).wait()
    for _, m_, c, n in order[LAST]:
        exchange.event(m_, c, n)
    exchange.end()


def backward(a1, a0, h1, dy, weights, w, m, v):
    tokens, d = a1.shape
    return pl.pallas_call(
        backward_kernel,
        in_specs=[ANY] * 7 + [VMEM] * 9,
        out_specs=[VMEM, ANY, ANY],
        out_shape=[*EXCHANGED, jax.ShapeDtypeStruct((6, 6, 4, 4, 4, 48, 128), BF16)],
        scratch_shapes=[
            pltpu.VMEM((tokens, d), BF16),
            pltpu.VMEM((tokens, d), BF16),
            pltpu.VMEM((tokens, d), F32),
            pltpu.VMEM((3, tokens, 512), BF16),
            pltpu.VMEM((2, d, 512), BF16),
            pltpu.VMEM((2, d, 512), BF16),
            pltpu.VMEM((2, 512, d), BF16),
            pltpu.VMEM((d, 512), F32),
            pltpu.VMEM((2, 4, 4, 4, 48, 128), BF16),
            pltpu.VMEM((6, 4, 4, 4, 48, 128), BF16),
            pltpu.SemaphoreType.DMA((2,)),
            pltpu.SemaphoreType.DMA((2, 3)),
            pltpu.SemaphoreType.DMA((3,)),
            *exchange_scratch(),
        ],
        compiler_params=pltpu.CompilerParams(collective_id=0, has_side_effects=True, vmem_limit_bytes=ALL_VMEM),
        name="backward",
    )(a1, a0, h1, dy, *weights, *w, *m, *v)


def results_kernel(*refs):
    full, sums, m, v = refs[0:2], refs[2:4], refs[4:7], refs[7:10]
    new_w, new_m, new_v = refs[10:13], refs[13:16], refs[16:19]
    for n in range(2):
        for j in range(6):
            columns = pl.ds(128 * j, 128)
            new_w[0][n, :, columns] = full[n][0, j].reshape(192, 128)
            for k in (1, 2):
                block = full[n][k, j].astype(F32)
                for q in range(4):
                    rows = jnp.concatenate([block[z, 12 * q : 12 * q + 12] for z in range(4)], axis=0)
                    new_w[k][n, :, pl.ds(512 * j + 128 * q, 128)] = rows.astype(BF16)

    @pl.when(pl.program_id(0) == 0)
    def _():
        for n in range(2):
            for j in range(6):
                for k in range(3):
                    for q in range(4 if k else 1):
                        g = sums[n][k, j, 12 * q : 12 * q + 12, :] if k else sums[n][k, j]
                        where = (n, slice(None), pl.ds(512 * j + 128 * q if k else 128 * j, 128))
                        new_m[k][where] = 0.9 * m[k][where] + 0.1 * g
                        new_v[k][where] = 0.95 * v[k][where] + 0.05 * g * g


def results(full, sums, m, v):
    def whole(t):
        return pl.BlockSpec(t.shape, lambda i: (0,) * t.ndim)

    full = [t.reshape(3, 6, 64, 48, 128) for t in full]
    part = pl.BlockSpec((3, 6, 4, 48, 128), lambda i: (0, 0, i, 0, 0))
    shapes = [(2, 3072, 768), (2, 768, 3072), (2, 768, 3072)]
    return pl.pallas_call(
        results_kernel,
        grid=(16,),
        in_specs=[part] * 2 + [whole(t) for t in (*sums, *m, *v)],
        out_specs=[pl.BlockSpec((2, s[1] // 16, s[2]), lambda i: (0, i, 0)) for s in shapes] + [whole(t) for t in (*m, *v)],
        out_shape=[jax.ShapeDtypeStruct(s, BF16) for s in shapes] + [jax.ShapeDtypeStruct(t.shape, F32) for t in (*m, *v)],
        compiler_params=pltpu.CompilerParams(vmem_limit_bytes=VMEM_LIMIT),
        name="results",
    )(*full, *sums, *m, *v)


def solution(mesh):
    def step(x, dy, w_gate, w_up, w_down, m_gate, m_up, m_down, v_gate, v_up, v_down):
        h0, dy = x[0], dy[0]
        me = lax.axis_index("dp")
        w = (w_down, w_gate, w_up)
        m, v = (m_down, m_gate, m_up), (v_down, v_gate, v_up)
        mine = [lax.dynamic_slice_in_dim(t, me * (t.shape[1] // 64), t.shape[1] // 64, 1) for t in w]

        a0 = normed(h0)
        gate = jnp.dot(a0, w_gate[0], preferred_element_type=F32)
        up = jnp.dot(a0, w_up[0], preferred_element_type=F32)
        h1 = h0 + matmul((jax.nn.silu(gate) * up).astype(BF16), w_down[0])
        a1 = normed(h1)
        sums1, full1, g = backward(a1, a0, h1, dy, (w_gate, w_up, w_down), mine, m, v)
        sums0, full0 = exchange(g, mine, m, v)
        new = results((full0, full1), (sums0, sums1), m, v)
        return tuple(new[3 * i + k] for i in range(3) for k in (1, 2, 0))

    rows = P(None, "dp", None)
    return jax.shard_map(
        step,
        mesh=mesh,
        in_specs=(P(("rep", "dp")),) * 2 + (P(),) * 3 + (rows,) * 6,
        out_specs=(P("rep"),) * 3 + (P("rep", "dp"),) * 6,
        check_vma=False,
    )
```

time: 586 us -> 453 us (0.77); the launches traced: 577 us -> 452 us
  matrix products: 184 us -> 45.7 us
  Pallas kernels: 367 us -> 380 us
    dot_general x4 -> x1, matrix products: 92.6 us -> 15.9 us  [step(): gate = jnp.dot(a0, w_gate[0], preferred_element_type=F32)]
    dot_general x5 -> x1, matrix products: 91.7 us -> 29.8 us  [matmul(): return jnp.dot(a, w, preferred_element_type=F32).astype(BF16)]
    pallas_call x8 -> x2, Pallas kernels: 340 us -> 353 us  [the longest x1 243 us: backward(): pl.pallas_call(backward_kernel, in_specs=[ANY] * 7 + [VMEM] * 9, out_spec...]
    unnamed x42 -> x14, local copies, waits for them, and re-layouts: 12.8 us -> 14 us
where the time goes in v2:
time: 453 us; the launch traced here: 452 us
  Pallas kernels  380 us (84%)
  matrix products  45.7 us (10%)
  local copies, waits for them, and re-layouts  17.5 us (4%)
  other arithmetic  8.56 us (2%)
    pallas_call x1, Pallas kernels, backward(): pl.pallas_call(backward_kernel, in_specs=[ANY] * 7 + [VMEM] * 9, out_spec...  243 us
    pallas_call x1, Pallas kernels, exchange(): pl.pallas_call(exchange_kernel, in_specs=[ANY] + [VMEM] * 9, out_specs=[V...  110 us
    dot_general x1, matrix products, matmul(): return jnp.dot(a, w, preferred_element_type=F32).astype(BF16)  29.8 us
    pallas_call x1, Pallas kernels, results(): pl.pallas_call(results_kernel, grid=(16,), in_specs=[part] * 2 + [whole(t...  26.9 us
    dot_general x1, matrix products, step(): gate = jnp.dot(a0, w_gate[0], preferred_element_type=F32)  15.9 us
    unnamed x14, local copies, waits for them, and re-layouts  14 us

profile of v2, /device:TPU:0, one launch (start us, length us, event | category | flops | bytes accessed | tf_op | source)
XLA Modules:
  0.0 452.2 jit_solution(17473661582670964930)
XLA Ops:
  0.6 0.0 copy-start.1
  0.7 0.0 copy-start.2
  0.7 2.7 fusion.1
  3.4 1.6 constant_dynamic-slice_fusion.2.refs_7_.refs_1_
  5.0 1.9 constant_dynamic-slice_fusion
  6.9 1.8 copy.21.refs_11_.refs_5_
  8.7 1.8 copy.22.refs_12_.refs_6_
  10.5 1.8 copy.23.refs_14_.refs_8_
  12.3 0.0 copy-done.2
  12.3 0.9 copy.24.refs_15_.refs_9_
  13.1 0.0 copy-done.1
  13.2 15.9 %fusion.8 = f32[2048,3072]{1,0:T(8,128)} fusion(bf16[2,768,3072]{2,1,0:T(8,128)(2,1)} %refs_4_.3, bf16[1,2048,768]{2,1,0:T(8,128)(2,1)S(1)} %copy-done.1, f32[2048]{0:T(1024)S(1)} %add_rsqrt_fusion.1), kind=kOutput, calls=%fused_computation.13 | convolution fusion | flops 9668395008 | bytes 33038336 | tf_op jit(solution)/shard_map/dot_general | solution.py:628
  29.0 29.8 %fusion.3 = (f32[2048]{0:T(1024)S(1)}, bf16[2048,768]{1,0:T(8,128)(2,1)S(1)}) fusion(bf16[2,3072,768]{2,1,0:T(8,128)(2,1)} %refs_6_.3, f32[2048,3072]{1,0:T(8,128)} %fusion.8, bf16[2,768,3072]{2,1,0:T(8,128)(2,1)} %refs_5_.3, bf16[1,2048,768]{2,1,0:T(8,128)(2,1)} %param.11, f32[2048]{0:T(1024)S(1)} %add_rsqrt_fusion.1), kind=kOutput, calls=%fused_computation.8 | convolution fusion | flops 19382401024 | bytes 44056576 | tf_op jit(solution)/shard_map/dot_general | solution.py:22
  58.9 0.0 copy-start
  58.9 5.8 %fusion.2 = (bf16[2048,768]{1,0:T(8,128)(2,1)}, bf16[2048,768]{1,0:T(8,128)(2,1)}) fusion(bf16[1,2048,768]{2,1,0:T(8,128)(2,1)} %param.11, f32[2048]{0:T(1024)S(1)} %add_rsqrt_fusion.1, f32[2048]{0:T(1024)S(1)} %add_rsqrt_fusion, bf16[2048,768]{1,0:T(8,128)(2,1)S(1)} %get-tuple-element.47.refs_2_), kind=kLoop, calls=%fused_computation.7 | loop fusion | flops 9437184 | bytes 12599296 | tf_op jit(solution)/shard_map/convert_element_type | solution.py:39
  64.7 0.0 copy-done
  64.7 243.2 %backward.1 = (f32[3,6,48,128]{3,2,1,0:T(8,128)}, bf16[3,6,4,4,4,48,128]{6,5,4,3,2,1,0:T(8,128)(2,1)}, bf16[6,6,4,4,4,48,128]{6,5,4,3,2,1,0:T(8,128)(2,1)}) custom-call(bf16[2048,768]{1,0:T(8,128)(2,1)} %get-tuple-element.51.refs_0_, bf16[2048,768]{1,0:T(8,128)(2,1)} %get-tuple-element.50.refs_1_, bf16[2048,768]{1,0:T(8,128)(2,1)} %copy-done, ...), custom_call_target="tpu_custom_call" | custom-call | tf_op jit(solution)/shard_map/backward/pallas_call | solution.py:550
  307.9 109.6 %exchange.1 = (f32[3,6,48,128]{3,2,1,0:T(8,128)}, bf16[3,6,4,4,4,48,128]{6,5,4,3,2,1,0:T(8,128)(2,1)}) custom-call(bf16[6,6,4,4,4,48,128]{6,5,4,3,2,1,0:T(8,128)(2,1)} %get-tuple-element.23.refs_0_, bf16[2,48,768]{2,1,0:T(8,128)(2,1)} %constant_dynamic-slice_fusion.2.refs_7_.refs_1_, bf16[2,12,3072]{2,1,0:T(8,128)(2,1)} %get-tuple-element.49.refs_8_.refs_2_, ...), custom_call_target="tpu_custom_call" | custom-call | tf_op jit(solution)/shard_map/exchange/pallas_call | solution.py:391
  417.5 26.9 %results.1 = (bf16[2,3072,768]{2,1,0:T(8,128)(2,1)}, bf16[2,768,3072]{2,1,0:T(8,128)(2,1)}, bf16[2,768,3072]{2,1,0:T(8,128)(2,1)}, f32[2,48,768]{2,1,0:T(8,128)}...) custom-call(bf16[3,6,64,48,128]{4,3,2,1,0:T(8,128)(2,1)} %bitcast.37, ...), custom_call_target="tpu_custom_call" | custom-call | tf_op jit(solution)/shard_map/results/pallas_call | solution.py:608
  444.4 1.9 copy.33
  446.3 1.9 copy.34
  448.3 1.9 copy.35
  450.2 1.9 copy.36
  (2 shorter events, 0.0 us)
Async XLA Ops:
  0.6 12.5 %copy-start.1 = (bf16[1,2048,768]{2,1,0:T(8,128)(2,1)S(1)}, bf16[1,2048,768]{2,1,0:T(8,128)(2,1)}, u32[]{:S(2)}) copy-start(bf16[1,2048,768]{2,1,0:T(8,128)(2,1)} %param.11) | copy-start | bytes 9437188
  0.7 11.6 %copy-start.2 = (f32[2,12,3072]{2,0,1:T(2,128)S(1)}, f32[2,12,3072]{2,0,1:T(2,128)}, u32[]{:S(2)}) copy-start(f32[2,12,3072]{2,0,1:T(2,128)} %param.20) | copy-start | bytes 884740
  58.9 5.8 %copy-start = (bf16[2048,768]{1,0:T(8,128)(2,1)}, bf16[2048,768]{1,0:T(8,128)(2,1)S(1)}, u32[]{:S(2)}) copy-start(bf16[2048,768]{1,0:T(8,128)(2,1)S(1)} %get-tuple-element.47.refs_2_) | copy-start | bytes 9437188

commit v3 on v2

--- a/solution.py
+++ b/solution.py
@@ -1,4 +1,5 @@
 import functools
+import itertools
 
 import jax
 import jax.numpy as jnp
@@ -12,18 +13,34 @@
 MESH = pl.DeviceIdType.MESH
 ANY = pl.BlockSpec(memory_space=pl.ANY)
 VMEM = pl.BlockSpec(memory_space=pltpu.VMEM)
+BLOCK = (48, 128)
+CHIPS = (4, 4, 4)
+STREAMS = 6
+WIDE = 512
 STRIDE = (16, 4, 1)
-ORDER = ((0, 1, 2), (1, 2, 0), (2, 0, 1))
+ORDER = tuple(tuple((i + k) % 3 for k in range(3)) for i in range(3))
 VMEM_LIMIT = 60 * 1024 * 1024
 ALL_VMEM = 67_043_328
 
 
-def matmul(a, w):
-    return jnp.dot(a, w, preferred_element_type=F32).astype(BF16)
-
-
 def over_tokens(a, b):
     return lax.dot_general(a, b, (((0,), (0,)), ((), ())), preferred_element_type=F32)
+
+
+def threes(refs):
+    return [refs[i : i + 3] for i in range(0, len(refs), 3)]
+
+
+def span(i, size):
+    return slice(size * i, size * i + size)
+
+
+def lanes(j):
+    return pl.ds(128 * j, 128)
+
+
+def quarter(j, q):
+    return pl.ds(WIDE * j + 128 * q, 128)
 
 
 def over_columns(a, b):
@@ -176,15 +193,18 @@
         n = self.layer
         self.sum[m, j] = g
         if m == 0:
-            where = (n, slice(None), pl.ds(128 * j, 128))
+            where = (n, slice(None), lanes(j))
             new = adamw(self.w[m][where].astype(F32), self.m[m][where], self.v[m][where], g)[0]
         else:
             self.scratch[0] = g
             for q in range(4):
-                rows = pl.ds(12 * q, 12)
-                where = (n, slice(None), pl.ds(512 * j + 128 * q, 128))
+                rows = span(q, 12)
+                columns = quarter(j, q)
                 self.scratch[1, rows, :] = adamw(
-                    self.w[m][where].astype(F32), self.m[m][where], self.v[m][where], self.scratch[0, rows, :]
+                    self.w[m][n, :, columns].astype(F32),
+                    self.m[m][:, n, columns],
+                    self.v[m][:, n, columns],
+                    self.scratch[0, rows, :],
                 )[0]
             new = self.scratch[1]
         self.new[m, j] = new.astype(BF16)
@@ -264,9 +284,8 @@
 UNITS, STEPS = 6, 7
 TURN = UNITS * STEPS
 LAST = 2 * TURN + 1
-STEP_US = {1: (3.2,) * 4 + (2.7, 2.7, 2.5), 0: (2.2,) * 4 + (2.7, 2.7, 2.5)}
-EVENT_US = (0.3, 0.8, 1.2, 0.3, 0.5, 0.2, 0.6, 0.2, 0.2, 0.2, 0.2, 0.2, 0.1)
-HALF_US, HOP_US, SLACK_US = 4.3, 2.5, 1.0
+STEP_US, EVENT_US = (2.1, 2.6), 0.3
+HALF_US, HOP_US, SLACK_US = 4.3, 2.5, 0.0
 
 
 def first_step(layer, m, c):
@@ -290,7 +309,7 @@
     def run(key, time):
         layer, m, c = key
         n = heads[key]
-        time += EVENT_US[n]
+        time += EVENT_US
         heads[key] = n + 1
         arrival = time
         if n < 6:
@@ -333,7 +352,7 @@
             order[step].append((*key, heads[key]))
             now = run(key, max(now, time))
         if step < last:
-            now += 4.0 if step == TURN else STEP_US[1 if step < TURN else 0][(step - (step > TURN)) % STEPS]
+            now += STEP_US[step <= TURN]
     return order, now
 
 
@@ -354,11 +373,11 @@
 
 
 def exchange_scratch():
-    shapes = [(3, 3, 2, 4, 4, 48, 128), (3, 3, 2, 4, 48, 128), (3, 3, 2, 48, 128)]
+    shapes = [(3, 3, 2, *CHIPS[i:], *BLOCK) for i in (1, 2, 3)]
     return [
-        pltpu.VMEM((3, 3, 2, 4, 4, 48, 128), BF16),
-        pltpu.VMEM((3, 6, 48, 128), BF16),
-        pltpu.VMEM((2, 48, 128), F32),
+        pltpu.VMEM(shapes[0], BF16),
+        pltpu.VMEM((3, STREAMS, *BLOCK), BF16),
+        pltpu.VMEM((2, *BLOCK), F32),
         *[pltpu.VMEM(s, BF16) for s in shapes for _ in range(3)],
         pltpu.SemaphoreType.DMA((9, 30)),
         pltpu.SemaphoreType.DMA((9, 30)),
@@ -369,22 +388,21 @@
 
 def exchange_of(layer, place, g, w, m, v, sums, full, scratch):
     own, new, small = scratch[:3]
-    bufs = [scratch[3 + 3 * i : 6 + 3 * i] for i in range(3)]
-    return Exchange(layer, place, (g, w, m, v, sums, full, new, bufs, own, small, *scratch[12:16]))
+    return Exchange(layer, place, (g, w, m, v, sums, full, new, threes(scratch[3:12]), own, small, *scratch[12:]))
 
 
 def exchange_kernel(*refs):
-    g_ref = refs[0]
-    w, m, v = refs[1:4], refs[4:7], refs[7:10]
+    g_ref, *refs = refs
+    w, m, v = threes(refs[:9])
     place = places()
-    exchange = exchange_of(0, place, g_ref, w, m, v, *refs[10:12], refs[12:])
+    exchange = exchange_of(0, place, g_ref, w, m, v, *refs[9:11], refs[11:])
     greet(place)
     for _, m_, c, n in schedule(0, 0)[0][0]:
         exchange.event(m_, c, n)
     exchange.end()
 
 
-EXCHANGED = [jax.ShapeDtypeStruct((3, 6, 48, 128), F32), jax.ShapeDtypeStruct((3, 6, 4, 4, 4, 48, 128), BF16)]
+EXCHANGED = [jax.ShapeDtypeStruct((3, STREAMS, *BLOCK), F32), jax.ShapeDtypeStruct((3, STREAMS, *CHIPS, *BLOCK), BF16)]
 
 
 def exchange(g, w, m, v):
@@ -401,7 +419,7 @@
 
 def backward_kernel(*refs):
     a1_ref, a0_ref, h1_ref, dy_ref, w_gate_ref, w_up_ref, w_down_ref = refs[:7]
-    w, m, v = refs[7:10], refs[10:13], refs[13:16]
+    w, m, v = threes(refs[7:16])
     sum_ref, full_ref, g_ref = refs[16:19]
     a_ref, d_ref, da_ref, tile_ref, wg_ref, wu_ref, wd_ref, s_ref, wide_ref, down_ref, load_sem, weight_sem, store_sem = refs[19:32]
     place = places()
@@ -409,7 +427,7 @@
 
     def weights(unit):
         layer, j, slot = 1 - lax.div(unit, UNITS), lax.rem(unit, UNITS), lax.rem(unit, 2)
-        some = pl.ds(pl.multiple_of(512 * j, 512), 512)
+        some = pl.ds(pl.multiple_of(WIDE * j, WIDE), WIDE)
         return (
             pltpu.make_async_copy(w_gate_ref.at[layer, :, some], wg_ref.at[slot], weight_sem.at[slot, 0]),
             pltpu.make_async_copy(w_up_ref.at[layer, :, some], wu_ref.at[slot], weight_sem.at[slot, 1]),
@@ -429,7 +447,7 @@
     greet(place)
 
     def tokens(layer, unit, block):
-        rows = pl.ds(pl.multiple_of(512 * block, 512), 512)
+        rows = pl.ds(pl.multiple_of(WIDE * block, WIDE), WIDE)
         slot = lax.rem(unit, 2)
         a, d = a_ref[rows, :], d_ref[rows, :]
         gate = jnp.dot(a, wg_ref[slot], preferred_element_type=F32)
@@ -456,7 +474,7 @@
         def two_devices(i, _):
             rows = s_ref[pl.ds(pl.multiple_of(24 * i, 8), 24), :]
             for k in range(2):
-                block = [rows[12 * k : 12 * k + 12, 128 * q : 128 * q + 128] for q in range(4)]
+                block = [rows[span(k, 12), span(q, 128)] for q in range(4)]
                 x, y, z = split(2 * i + k)
                 wide_ref[which, x, y, z] = jnp.concatenate(block, axis=0).astype(BF16)
             return 0
@@ -477,7 +495,7 @@
             x, y, z = split(lax.div(32 * j + i, 3))
             rows = pl.ds(pl.multiple_of(16 * lax.rem(32 * j + i, 3), 16), 16)
             for k in range(6):
-                down_ref[k, x, y, z, rows, :] = total[16 * i : 16 * i + 16, 128 * k : 128 * k + 128].astype(BF16)
+                down_ref[k, x, y, z, rows, :] = total[span(i, 16), span(k, 128)].astype(BF16)
         store_wide(layer, j, 1).wait()
 
         @pl.when(j == UNITS - 1)
@@ -551,7 +569,7 @@
         backward_kernel,
         in_specs=[ANY] * 7 + [VMEM] * 9,
         out_specs=[VMEM, ANY, ANY],
-        out_shape=[*EXCHANGED, jax.ShapeDtypeStruct((6, 6, 4, 4, 4, 48, 128), BF16)],
+        out_shape=[*EXCHANGED, jax.ShapeDtypeStruct((6, STREAMS, *CHIPS, *BLOCK), BF16)],
         scratch_shapes=[
             pltpu.VMEM((tokens, d), BF16),
             pltpu.VMEM((tokens, d), BF16),
@@ -561,8 +579,8 @@
             pltpu.VMEM((2, d, 512), BF16),
             pltpu.VMEM((2, 512, d), BF16),
             pltpu.VMEM((d, 512), F32),
-            pltpu.VMEM((2, 4, 4, 4, 48, 128), BF16),
-            pltpu.VMEM((6, 4, 4, 4, 48, 128), BF16),
+            pltpu.VMEM((2, *CHIPS, *BLOCK), BF16),
+            pltpu.VMEM((STREAMS, *CHIPS, *BLOCK), BF16),
             pltpu.SemaphoreType.DMA((2,)),
             pltpu.SemaphoreType.DMA((2, 3)),
             pltpu.SemaphoreType.DMA((3,)),
@@ -574,17 +592,16 @@
 
 
 def results_kernel(*refs):
-    full, sums, m, v = refs[0:2], refs[2:4], refs[4:7], refs[7:10]
-    new_w, new_m, new_v = refs[10:13], refs[13:16], refs[16:19]
-    for n in range(2):
-        for j in range(6):
-            columns = pl.ds(128 * j, 128)
-            new_w[0][n, :, columns] = full[n][0, j].reshape(192, 128)
-            for k in (1, 2):
-                block = full[n][k, j].astype(F32)
-                for q in range(4):
-                    rows = jnp.concatenate([block[z, 12 * q : 12 * q + 12] for z in range(4)], axis=0)
-                    new_w[k][n, :, pl.ds(512 * j + 128 * q, 128)] = rows.astype(BF16)
+    full, sums = refs[:2], refs[2:4]
+    m, v, new_w, new_m, new_v = threes(refs[4:])
+    for n, part, j in itertools.product(range(2), range(2), range(6)):
+        devices = span(part, 4)
+        new_w[0][n, span(part, 192), lanes(j)] = full[n][0, j, devices].reshape(192, 128)
+        for k in (1, 2):
+            block = full[n][k, j, devices].astype(F32)
+            for q in range(4):
+                rows = jnp.concatenate([block[z, span(q, 12)] for z in range(4)], axis=0)
+                new_w[k][n, span(part, 48), quarter(j, q)] = rows.astype(BF16)
 
     @pl.when(pl.program_id(0) == 0)
     def _():
@@ -592,47 +609,80 @@
             for j in range(6):
                 for k in range(3):
                     for q in range(4 if k else 1):
-                        g = sums[n][k, j, 12 * q : 12 * q + 12, :] if k else sums[n][k, j]
-                        where = (n, slice(None), pl.ds(512 * j + 128 * q if k else 128 * j, 128))
+                        g = sums[n][k, j, span(q, 12), :] if k else sums[n][k, j]
+                        where = (slice(None), n, quarter(j, q)) if k else (n, slice(None), lanes(j))
                         new_m[k][where] = 0.9 * m[k][where] + 0.1 * g
                         new_v[k][where] = 0.95 * v[k][where] + 0.05 * g * g
 
 
-def results(full, sums, m, v):
+def results(full, sums, w, m, v):
     def whole(t):
         return pl.BlockSpec(t.shape, lambda i: (0,) * t.ndim)
 
-    full = [t.reshape(3, 6, 64, 48, 128) for t in full]
-    part = pl.BlockSpec((3, 6, 4, 48, 128), lambda i: (0, 0, i, 0, 0))
-    shapes = [(2, 3072, 768), (2, 768, 3072), (2, 768, 3072)]
+    full = [t.reshape(3, STREAMS, 64, *BLOCK) for t in full]
+    part = pl.BlockSpec((3, STREAMS, 8, *BLOCK), lambda i: (0, 0, i, 0, 0))
+    shapes = [t.shape for t in w]
     return pl.pallas_call(
         results_kernel,
-        grid=(16,),
+        grid=(8,),
         in_specs=[part] * 2 + [whole(t) for t in (*sums, *m, *v)],
-        out_specs=[pl.BlockSpec((2, s[1] // 16, s[2]), lambda i: (0, i, 0)) for s in shapes] + [whole(t) for t in (*m, *v)],
+        out_specs=[pl.BlockSpec((2, s[1] // 8, s[2]), lambda i: (0, i, 0)) for s in shapes] + [whole(t) for t in (*m, *v)],
         out_shape=[jax.ShapeDtypeStruct(s, BF16) for s in shapes] + [jax.ShapeDtypeStruct(t.shape, F32) for t in (*m, *v)],
         compiler_params=pltpu.CompilerParams(vmem_limit_bytes=VMEM_LIMIT),
         name="results",
     )(*full, *sums, *m, *v)
 
 
+def forward_kernel(x_ref, w_gate_ref, w_up_ref, w_down_ref, a0_ref, h1_ref, a1_ref, total_ref):
+    a0_ref[...] = normed(x_ref[0])
+    total_ref[...] = jnp.zeros_like(total_ref)
+
+    def unit(j, _):
+        some = pl.ds(pl.multiple_of(WIDE * j, WIDE), WIDE)
+        gate = jnp.dot(a0_ref[...], w_gate_ref[0, :, some], preferred_element_type=F32)
+        up = jnp.dot(a0_ref[...], w_up_ref[0, :, some], preferred_element_type=F32)
+        act = (jax.nn.silu(gate) * up).astype(BF16)
+        total_ref[...] += jnp.dot(act, w_down_ref[0, some, :], preferred_element_type=F32)
+        return 0
+
+    lax.fori_loop(0, UNITS, unit, 0)
+    h1 = x_ref[0] + total_ref[...].astype(BF16)
+    h1_ref[...] = h1
+    a1_ref[...] = normed(h1)
+
+
+def forward(x, *weights):
+    _, tokens, d = x.shape
+    rows = pl.BlockSpec((WIDE, d), lambda i: (i, 0))
+    return pl.pallas_call(
+        forward_kernel,
+        grid=(tokens // WIDE,),
+        in_specs=[pl.BlockSpec((1, WIDE, d), lambda i: (0, i, 0))] + [pl.BlockSpec((1, *t.shape[1:]), lambda i: (0, 0, 0)) for t in weights],
+        out_specs=[rows] * 3,
+        out_shape=[jax.ShapeDtypeStruct((tokens, d), BF16)] * 3,
+        scratch_shapes=[pltpu.VMEM((WIDE, d), F32)],
+        compiler_params=pltpu.CompilerParams(vmem_limit_bytes=VMEM_LIMIT),
+        name="forward",
+    )(x, *weights)
+
+
+def rows_first(t):
+    return jnp.transpose(t, (1, 0, 2))
+
+
 def solution(mesh):
     def step(x, dy, w_gate, w_up, w_down, m_gate, m_up, m_down, v_gate, v_up, v_down):
-        h0, dy = x[0], dy[0]
+        dy = dy[0]
         me = lax.axis_index("dp")
         w = (w_down, w_gate, w_up)
-        m, v = (m_down, m_gate, m_up), (v_down, v_gate, v_up)
+        m, v = ((t[0], *(rows_first(o) for o in t[1:])) for t in ((m_down, m_gate, m_up), (v_down, v_gate, v_up)))
         mine = [lax.dynamic_slice_in_dim(t, me * (t.shape[1] // 64), t.shape[1] // 64, 1) for t in w]
 
-        a0 = normed(h0)
-        gate = jnp.dot(a0, w_gate[0], preferred_element_type=F32)
-        up = jnp.dot(a0, w_up[0], preferred_element_type=F32)
-        h1 = h0 + matmul((jax.nn.silu(gate) * up).astype(BF16), w_down[0])
-        a1 = normed(h1)
+        a0, h1, a1 = forward(x, w_gate, w_up, w_down)
         sums1, full1, g = backward(a1, a0, h1, dy, (w_gate, w_up, w_down), mine, m, v)
         sums0, full0 = exchange(g, mine, m, v)
-        new = results((full0, full1), (sums0, sums1), m, v)
-        return tuple(new[3 * i + k] for i in range(3) for k in (1, 2, 0))
+        new = results((full0, full1), (sums0, sums1), w, m, v)
+        return tuple(rows_first(new[3 * i + k]) if i and k else new[3 * i + k] for i in range(3) for k in (1, 2, 0))
 
     rows = P(None, "dp", None)
     return jax.shard_map(

time: 453 us -> 421 us (0.929)
  matrix products: 45.7 us -> 0 us
  Pallas kernels: 380 us -> 417 us
  local copies, waits for them, and re-layouts: 17.5 us -> 3.49 us
  other arithmetic: 8.56 us -> 0 us
    dot_general x2 -> x0, matrix products: 45.7 us -> none  [the longest x1 29.8 us: matmul(): return jnp.dot(a, w, preferred_element_type=F32).astype(BF16)]
    pallas_call x1 -> x2, Pallas kernels: 26.9 us -> 70.3 us  [the longest x1 46.1 us: forward(): pl.pallas_call(forward_kernel, grid=(tokens // WIDE,), in_specs=[pl.Block...]
    unnamed x14 -> x0, local copies, waits for them, and re-layouts: 14 us -> none
    convert_element_type x1 -> x0, other arithmetic: 5.81 us -> none  [normed(): return (wide * scale_of(wide)).astype(BF16)]
where the time goes in v3:
time: 421 us
  Pallas kernels  417 us (99%)
    pallas_call x1, Pallas kernels, backward(): pl.pallas_call(backward_kernel, in_specs=[ANY] * 7 + [VMEM] * 9, out_spec...  240 us
    pallas_call x1, Pallas kernels, exchange(): pl.pallas_call(exchange_kernel, in_specs=[ANY] + [VMEM] * 9, out_specs=[V...  106 us
    pallas_call x1, Pallas kernels, forward(): pl.pallas_call(forward_kernel, grid=(tokens // WIDE,), in_specs=[pl.Block...  46.1 us
    pallas_call x1, Pallas kernels, results(): pl.pallas_call(results_kernel, grid=(8,), in_specs=[part] * 2 + [whole(t)...  24.2 us

profile of v3, /device:TPU:0, one launch (start us, length us, event | category | flops | bytes accessed | tf_op | source)
XLA Modules:
  0.0 421.2 jit_solution(5684014297249656620)
XLA Ops:
  0.6 1.6 constant_dynamic-slice_fusion.2.refs_7_.refs_1_
  2.2 1.9 constant_dynamic-slice_fusion
  4.1 46.1 %forward.1 = (bf16[2048,768]{1,0:T(8,128)(2,1)}, bf16[2048,768]{1,0:T(8,128)(2,1)}, bf16[2048,768]{1,0:T(8,128)(2,1)}) custom-call(bf16[1,2048,768]{2,1,0:T(8,128)(2,1)} %x_ref.1, bf16[2,768,3072]{2,1,0:T(8,128)(2,1)} %refs_4_.3, bf16[2,768,3072]{2,1,0:T(8,128)(2,1)} %refs_5_.1, bf16[2,3072,768]{2,1,0:T(8,128)(2,1)} %refs_6_.1), custom_call_target="tpu_custom_call" | custom-call | tf_op jit(solution)/shard_map/forward/pallas_call | solution.py:657
  50.2 240.2 %backward.1 = (f32[3,6,48,128]{3,2,1,0:T(8,128)}, bf16[3,6,4,4,4,48,128]{6,5,4,3,2,1,0:T(8,128)(2,1)}, bf16[6,6,4,4,4,48,128]{6,5,4,3,2,1,0:T(8,128)(2,1)}) custom-call(bf16[2048,768]{1,0:T(8,128)(2,1)} %get-tuple-element.26.refs_0_, bf16[2048,768]{1,0:T(8,128)(2,1)} %get-tuple-element.27.refs_1_, bf16[2048,768]{1,0:T(8,128)(2,1)} %get-tuple-element.28.refs_2_, ...), custom_call_target="tpu_custom_call" | custom-call | tf_op jit(solution)/shard_map/backward/pallas_call | solution.py:568
  290.4 106.3 %exchange.1 = (f32[3,6,48,128]{3,2,1,0:T(8,128)}, bf16[3,6,4,4,4,48,128]{6,5,4,3,2,1,0:T(8,128)(2,1)}) custom-call(bf16[6,6,4,4,4,48,128]{6,5,4,3,2,1,0:T(8,128)(2,1)} %get-tuple-element.29.refs_0_, bf16[2,48,768]{2,1,0:T(8,128)(2,1)} %constant_dynamic-slice_fusion.2.refs_7_.refs_1_, bf16[2,12,3072]{2,1,0:T(8,128)(2,1)} %get-tuple-element.44.refs_8_.refs_2_, ...), custom_call_target="tpu_custom_call" | custom-call | tf_op jit(solution)/shard_map/exchange/pallas_call | solution.py:409
  396.7 24.2 %results.1 = (bf16[2,3072,768]{2,1,0:T(8,128)(2,1)}, bf16[2,768,3072]{2,1,0:T(8,128)(2,1)}, bf16[2,768,3072]{2,1,0:T(8,128)(2,1)}, f32[2,48,768]{2,1,0:T(8,128)}...) custom-call(bf16[3,6,64,48,128]{4,3,2,1,0:T(8,128)(2,1)} %bitcast.12, ...), custom_call_target="tpu_custom_call" | custom-call | tf_op jit(solution)/shard_map/results/pallas_call | solution.py:625

commit v4 on v3

--- a/solution.py
+++ b/solution.py
@@ -469,17 +469,12 @@
         return pltpu.make_async_copy(wide_ref.at[which], g_ref.at[3 * layer + 1 + which, j], store_sem.at[which])
 
     def wide(layer, j, which):
-        s_ref[...] = over_tokens(a_ref[...], tile_ref[1 + which])
-
-        def two_devices(i, _):
-            rows = s_ref[pl.ds(pl.multiple_of(24 * i, 8), 24), :]
-            for k in range(2):
-                block = [rows[span(k, 12), span(q, 128)] for q in range(4)]
-                x, y, z = split(2 * i + k)
-                wide_ref[which, x, y, z] = jnp.concatenate(block, axis=0).astype(BF16)
-            return 0
-
-        lax.fori_loop(0, 32, two_devices, 0)
+        halves = s_ref.shape[0] // 2
+        for half in range(2):
+            s_ref[span(half, halves), :] = over_tokens(a_ref[:, span(half, halves)], tile_ref[1 + which])
+        for d in range(64):
+            block = [s_ref[span(d, 12), span(q, 128)] for q in range(4)]
+            wide_ref[which, d // 16, d // 4 % 4, d % 4] = jnp.concatenate(block, axis=0).astype(BF16)
         store_wide(layer, j, which).start()
 
         @pl.when(which == 1)
@@ -645,7 +640,7 @@
         total_ref[...] += jnp.dot(act, w_down_ref[0, some, :], preferred_element_type=F32)
         return 0
 
-    lax.fori_loop(0, UNITS, unit, 0)
+    lax.fori_loop(0, UNITS, unit, 0, unroll=2)
     h1 = x_ref[0] + total_ref[...].astype(BF16)
     h1_ref[...] = h1
     a1_ref[...] = normed(h1)

time: 421 us -> 407 us (0.967)
  Pallas kernels: 417 us -> 403 us
    pallas_call x1, Pallas kernels: 240 us -> 229 us  [backward(): pl.pallas_call(backward_kernel, in_specs=[ANY] * 7 + [VMEM] * 9, out_spec...]
where the time goes in v4:
time: 407 us
  Pallas kernels  403 us (99%)
    pallas_call x1, Pallas kernels, backward(): pl.pallas_call(backward_kernel, in_specs=[ANY] * 7 + [VMEM] * 9, out_spec...  229 us
    pallas_call x1, Pallas kernels, exchange(): pl.pallas_call(exchange_kernel, in_specs=[ANY] + [VMEM] * 9, out_specs=[V...  104 us
    pallas_call x1, Pallas kernels, forward(): pl.pallas_call(forward_kernel, grid=(tokens // WIDE,), in_specs=[pl.Block...  45.6 us
    pallas_call x1, Pallas kernels, results(): pl.pallas_call(results_kernel, grid=(8,), in_specs=[part] * 2 + [whole(t)...  24.2 us

profile of v4, /device:TPU:0, one launch (start us, length us, event | category | flops | bytes accessed | tf_op | source)
XLA Modules:
  0.0 406.9 jit_solution(11350417047728739856)
XLA Ops:
  0.6 1.6 constant_dynamic-slice_fusion.2.refs_7_.refs_1_
  2.2 1.9 constant_dynamic-slice_fusion
  4.1 45.6 %forward.1 = (bf16[2048,768]{1,0:T(8,128)(2,1)}, bf16[2048,768]{1,0:T(8,128)(2,1)}, bf16[2048,768]{1,0:T(8,128)(2,1)}) custom-call(bf16[1,2048,768]{2,1,0:T(8,128)(2,1)} %x_ref.1, bf16[2,768,3072]{2,1,0:T(8,128)(2,1)} %refs_4_.3, bf16[2,768,3072]{2,1,0:T(8,128)(2,1)} %refs_5_.1, bf16[2,3072,768]{2,1,0:T(8,128)(2,1)} %refs_6_.1), custom_call_target="tpu_custom_call" | custom-call | tf_op jit(solution)/shard_map/forward/pallas_call | solution.py:652
  49.7 228.8 %backward.1 = (f32[3,6,48,128]{3,2,1,0:T(8,128)}, bf16[3,6,4,4,4,48,128]{6,5,4,3,2,1,0:T(8,128)(2,1)}, bf16[6,6,4,4,4,48,128]{6,5,4,3,2,1,0:T(8,128)(2,1)}) custom-call(bf16[2048,768]{1,0:T(8,128)(2,1)} %get-tuple-element.26.refs_0_, bf16[2048,768]{1,0:T(8,128)(2,1)} %get-tuple-element.27.refs_1_, bf16[2048,768]{1,0:T(8,128)(2,1)} %get-tuple-element.28.refs_2_, ...), custom_call_target="tpu_custom_call" | custom-call | tf_op jit(solution)/shard_map/backward/pallas_call | solution.py:563
  278.5 104.0 %exchange.1 = (f32[3,6,48,128]{3,2,1,0:T(8,128)}, bf16[3,6,4,4,4,48,128]{6,5,4,3,2,1,0:T(8,128)(2,1)}) custom-call(bf16[6,6,4,4,4,48,128]{6,5,4,3,2,1,0:T(8,128)(2,1)} %get-tuple-element.29.refs_0_, bf16[2,48,768]{2,1,0:T(8,128)(2,1)} %constant_dynamic-slice_fusion.2.refs_7_.refs_1_, bf16[2,12,3072]{2,1,0:T(8,128)(2,1)} %get-tuple-element.44.refs_8_.refs_2_, ...), custom_call_target="tpu_custom_call" | custom-call | tf_op jit(solution)/shard_map/exchange/pallas_call | solution.py:409
  382.5 24.2 %results.1 = (bf16[2,3072,768]{2,1,0:T(8,128)(2,1)}, bf16[2,768,3072]{2,1,0:T(8,128)(2,1)}, bf16[2,768,3072]{2,1,0:T(8,128)(2,1)}, f32[2,48,768]{2,1,0:T(8,128)}...) custom-call(bf16[3,6,64,48,128]{4,3,2,1,0:T(8,128)(2,1)} %bitcast.12, ...), custom_call_target="tpu_custom_call" | custom-call | tf_op jit(solution)/shard_map/results/pallas_call | solution.py:620
